TPU v7x, 16 devices: a whole 2x2x2 slice. The times are simulated.
16 devices in a mesh: tp: 4 (over z, y), dp: 4 (over x, core).
Axes of the slice: x: 2, y: 2, z: 2, core: 2. Of those that a mesh axis runs over, the one named last changes fastest.
Arguments:
- x: bfloat16 [512, 2048], P('dp')
- lengths: int32 [512], P('dp')
- cache: bfloat16 [2, 512, 512, 576], P(None, 'dp')
- attn_norm: bfloat16 [2, 2048], replicated
- ffn_norm: bfloat16 [2, 2048], replicated
- wq: bfloat16 [2, 2048, 9216], P(None, None, 'tp')
- wo: bfloat16 [2, 8192, 2048], P(None, 'tp')
- w1: bfloat16 [2, 2048, 10944], P(None, None, ('dp', 'tp'))
- w3: bfloat16 [2, 2048, 10944], P(None, None, ('dp', 'tp'))
- w2: bfloat16 [2, 10944, 2048], P(None, ('dp', 'tp'))
Outputs:
- output: bfloat16 [512, 2048], P('dp')
All inputs are finite; a program needn't handle non-finite values.
Results may differ from a plain program's by a relative error of at most 0.02.
Values are sent between devices in bfloat16 or wider.
A program may use at most 1 GiB of HBM per device.

v0:
```python
import jax
import jax.numpy as jnp
from jax import lax
from jax.sharding import PartitionSpec as P

LAT = 512
EPS = 1e-6
SCALE = 192 ** -0.5


def _rmsnorm(v, w):
    vf = v.astype(jnp.float32)
    r = lax.rsqrt(jnp.mean(vf * vf, axis=-1, keepdims=True) + EPS)
    return (vf * r * w.astype(jnp.float32)).astype(jnp.bfloat16)


def solution(mesh):
    def body(x, lengths, cache, attn_norm, ffn_norm, wq, wo, w1, w3, w2):
        nb = x.shape[0]
        n_layers, _, s_len, kv = cache.shape
        nh = wq.shape[2] // kv
        keep = (jnp.arange(s_len)[None, :] < lengths[:, None])[:, None, :]
        for l in range(n_layers):
            c = cache[l]
            h = _rmsnorm(x, attn_norm[l])
            q = jnp.dot(h, wq[l], preferred_element_type=jnp.float32).astype(jnp.bfloat16).reshape(nb, nh, kv)
            s = jnp.einsum('bhk,btk->bht', q, c, preferred_element_type=jnp.float32) * SCALE
            p = jax.nn.softmax(jnp.where(keep, s, -jnp.inf), axis=-1).astype(jnp.bfloat16)
            o = jnp.einsum('bht,btk->bhk', p, c[:, :, :LAT], preferred_element_type=jnp.float32)
            o = o.astype(jnp.bfloat16).reshape(nb, nh * LAT)
            attn = lax.psum(jnp.dot(o, wo[l], preferred_element_type=jnp.float32), 'tp')
            x = x + attn.astype(jnp.bfloat16)
            g = _rmsnorm(x, ffn_norm[l])
            gg = lax.all_gather(g, 'dp', axis=0, tiled=True)
            u = jnp.dot(gg, w3[l], preferred_element_type=jnp.float32)
            v = jnp.dot(gg, w1[l], preferred_element_type=jnp.float32)
            a = (jax.nn.silu(u) * v).astype(jnp.bfloat16)
            yp = jnp.dot(a, w2[l], preferred_element_type=jnp.float32)
            y = lax.psum_scatter(yp, 'dp', scatter_dimension=0, tiled=True)
            y = lax.psum(y, 'tp')
            x = x + y.astype(jnp.bfloat16)
        return x

    in_specs = (
        P('dp', None),
        P('dp'),
        P(None, 'dp', None, None),
        P(None, None),
        P(None, None),
        P(None, None, 'tp'),
        P(None, 'tp', None),
        P(None, None, ('dp', 'tp')),
        P(None, None, ('dp', 'tp')),
        P(None, ('dp', 'tp'), None),
    )
    return jax.shard_map(body, mesh=mesh, in_specs=in_specs, out_specs=P('dp', None), check_vma=False)
```

profile of v0, /device:TPU:0, one launch (start us, length us, event | category | flops | bytes accessed | tf_op | source)
XLA Modules:
  0.0 581.5 jit_solution(17095298199049133599)
XLA Ops:
  6.5 0.0 all-gather.3.cloned.1.call-start
  6.5 1.4 slice_convert_fusion.1
  7.9 1.2 fusion.46
  9.1 0.0 copy-start.3
  9.2 5.3 fusion.18
  14.5 0.3 copy.13
  14.8 0.8 copy.14
  15.6 0.0 copy-done.3
  15.6 0.1 iota_compare_fusion
  15.7 97.1 %slice_bitcast_fusion = (bf16[128,512,576]{1,2,0:T(8,128)(2,1)}, bf16[128,512,576]{1,2,0:T(8,128)(2,1)}) fusion(bf16[2,128,512,576]{2,3,1,0:T(8,128)(2,1)} %param.12), kind=kLoop, calls=%fused_computation.2 | loop fusion | bytes 301989888 | tf_op jit(solution)/shard_map/squeeze | solution.py:24
  112.8 25.5 %fusion.73 = (f32[128,4]{1,0:T(8,128)S(1)}, f32[128,4,512]{2,1,0:T(4,128)S(1)}) fusion(bf16[128,4,576]{2,1,0:T(4,128)(2,1)S(1)} %copy.14, pred[128,512]{1,0:T(8,128)(4,1)S(1)} %iota_compare_fusion, bf16[2,128,512,576]{2,3,1,0:T(8,128)(2,1)} %param.12), kind=kOutput, calls=%fused_computation.96 | convolution fusion | flops 303038976 | bytes 77203456 | tf_op jit(solution)/shard_map/sub | solution.py:28
  138.3 25.5 %fusion.40 = bf16[128,4,512]{2,1,0:T(4,128)(2,1)S(1)} fusion(bf16[128,512,576]{1,2,0:T(8,128)(2,1)} %get-tuple-element.12, f32[128,4,512]{2,1,0:T(4,128)S(1)} %get-tuple-element.24, f32[128,4]{1,0:T(8,128)S(1)} %get-tuple-element.23), kind=kOutput, calls=%fused_computation.54 | convolution fusion | flops 269221888 | bytes 68683776 | tf_op jit(solution)/shard_map/bht,btk->bhk/dot_general | solution.py:29
  163.8 0.1 copy.33
  163.9 0.0 copy-start
  163.9 0.0 copy-start.1
  163.9 4.7 fusion.14
  168.7 42.7 %all-reduce.4 = bf16[128,2048]{1,0:T(8,128)(2,1)S(1)} all-reduce(f32[128,2048]{1,0:T(8,128)S(1)} %fusion.14), channel_id=1, replica_groups=mesh['tp'=4,'dp'=4] {'tp'}, use_global_device_ids=true, to_apply=%region_3.4 | all-reduce | flops 262144 | bytes 1572864 | tf_op jit(solution)/shard_map/psum | solution.py:31
  211.4 0.0 copy-done
  211.4 0.3 fusion.49
  211.7 0.0 copy-done.1
  211.7 1.0 fusion.51
  212.7 0.0 all-gather.3.cloned.1.call-update
  212.7 0.2 reduce-scatter.3.cloned.1.call-start
  213.0 0.0 slice-start
  213.0 14.6 %fusion.70 = (bf16[1,2048,684]{1,0,2:T(2,128)(2,1)}, bf16[1,2048,684]{1,0,2:T(2,128)(2,1)}) fusion(bf16[2,2048,684]{1,0,2:T(2,128)(2,1)} %param.18), kind=kLoop, calls=%fused_computation.93 | loop fusion | bytes 11206656 | tf_op jit(solution)/shard_map/slice | solution.py:35
  227.5 0.0 slice-start.1
  227.5 14.7 %fusion.71 = (bf16[1,2048,684]{1,0,2:T(2,128)(2,1)}, bf16[1,2048,684]{1,0,2:T(2,128)(2,1)}) fusion(bf16[2,2048,684]{1,0,2:T(2,128)(2,1)} %param.17), kind=kLoop, calls=%fused_computation.94 | loop fusion | bytes 11206656 | tf_op jit(solution)/shard_map/slice | solution.py:36
  242.2 0.0 slice-done
  242.2 0.0 slice-done.1
  242.2 9.1 %fusion.72 = (bf16[1,684,2048]{2,0,1:T(2,128)(2,1)}, bf16[1,684,2048]{2,0,1:T(2,128)(2,1)}) fusion(bf16[2,684,2048]{2,0,1:T(2,128)(2,1)S(1)} %bitcast.75), kind=kLoop, calls=%fused_computation.95 | loop fusion | bytes 11206656 | tf_op jit(solution)/shard_map/slice | solution.py:38
  251.3 0.0 all-gather.3.cloned.1.call-done
  251.3 0.0 copy-start.4
  251.3 6.4 %fusion.29 = f32[512,684]{0,1:T(8,128)} fusion(bf16[512,2048]{1,0:T(8,128)(2,1)} %all-gather.3.cloned.1.call-done, bf16[1,2048,684]{1,0,2:T(2,128)(2,1)} %get-tuple-element.14), kind=kOutput, calls=%fused_computation.33 | convolution fusion | flops 1434451968 | bytes 6299648 | tf_op jit(solution)/shard_map/dot_general | solution.py:35
  257.7 0.0 copy-done.4
  257.7 10.9 %fusion.27 = f32[512,2048]{1,0:T(8,128)} fusion(bf16[1,684,2048]{2,0,1:T(2,128)(2,1)} %get-tuple-element.18, bf16[512,2048]{1,0:T(8,128)(2,1)S(1)} %copy-done.4, bf16[1,2048,684]{1,0,2:T(2,128)(2,1)} %get-tuple-element.16, f32[512,684]{0,1:T(8,128)} %fusion.29), kind=kOutput, calls=%fused_computation.29 | convolution fusion | flops 2871005184 | bytes 13295616 | tf_op jit(solution)/shard_map/dot_general | solution.py:38
  268.6 0.0 copy-start.2
  268.6 0.0 reduce-scatter.3.cloned.1.call-update
  268.6 0.0 all-gather.5.cloned.1.call-start
  268.7 40.7 %reduce-scatter.3.cloned.1.call-done = f32[128,2048]{1,0:T(8,128)} async-done(((f32[512,2048]{1,0:T(8,128)}), f32[128,2048]{1,0:T(8,128)}) %reduce-scatter.3.cloned.1.call-update) | async-done | bytes 1048592 | tf_op jit(solution)/shard_map/reduce_scatter | solution.py:39
  309.4 41.4 %all-reduce.5 = bf16[128,2048]{1,0:T(8,128)(2,1)S(1)} all-reduce(f32[128,2048]{1,0:T(8,128)} %reduce-scatter.3.cloned.1.call-done), channel_id=1, replica_groups=mesh['tp'=4,'dp'=4] {'tp'}, use_global_device_ids=true, to_apply=%region_6.7 | all-reduce | flops 262144 | bytes 1572864 | tf_op jit(solution)/shard_map/psum | solution.py:40
  350.8 0.3 fusion.52
  351.1 0.0 copy-done.2
  351.2 5.1 fusion.21
  356.3 0.3 copy.19
  356.6 0.8 copy.20
  357.4 25.5 %fusion.74 = (f32[128,4]{1,0:T(8,128)S(1)}, f32[128,4,512]{2,1,0:T(4,128)S(1)}) fusion(bf16[128,4,576]{2,1,0:T(4,128)(2,1)S(1)} %copy.20, pred[128,512]{1,0:T(8,128)(4,1)S(1)} %iota_compare_fusion, bf16[2,128,512,576]{2,3,1,0:T(8,128)(2,1)} %param.12), kind=kOutput, calls=%fused_computation.97 | convolution fusion | flops 303038976 | bytes 77203456 | tf_op jit(solution)/shard_map/sub | solution.py:28
  382.9 25.5 %fusion.43 = bf16[128,4,512]{2,1,0:T(4,128)(2,1)S(1)} fusion(bf16[128,512,576]{1,2,0:T(8,128)(2,1)} %get-tuple-element.11, f32[128,4,512]{2,1,0:T(4,128)S(1)} %get-tuple-element.26, f32[128,4]{1,0:T(8,128)S(1)} %get-tuple-element.25), kind=kOutput, calls=%fused_computation.55 | convolution fusion | flops 269221888 | bytes 68683776 | tf_op jit(solution)/shard_map/bht,btk->bhk/dot_general | solution.py:29
  408.4 0.1 copy.34
  408.5 4.7 fusion.12
  413.2 41.1 %all-reduce.6 = bf16[128,2048]{1,0:T(8,128)(2,1)S(1)} all-reduce(f32[128,2048]{1,0:T(8,128)S(1)} %fusion.12), channel_id=1, replica_groups=mesh['tp'=4,'dp'=4] {'tp'}, use_global_device_ids=true, to_apply=%region_10.11 | all-reduce | flops 262144 | bytes 1572864 | tf_op jit(solution)/shard_map/psum | solution.py:31
  454.3 0.3 fusion.55
  454.6 1.0 fusion.57
  455.6 0.0 all-gather.5.cloned.1.call-update
  455.6 0.3 reduce-scatter.5.cloned.1.call-start
  455.9 19.4 %all-gather.5.cloned.1.call-done = bf16[512,2048]{1,0:T(8,128)(2,1)} async-done(((bf16[128,2048]{1,0:T(8,128)(2,1)}), bf16[512,2048]{1,0:T(8,128)(2,1)}) %all-gather.5.cloned.1.call-update) | async-done | bytes 2097168 | tf_op jit(solution)/shard_map/all_gather | solution.py:34
  475.3 0.0 copy-start.5
  475.3 6.4 %fusion.26 = f32[512,684]{0,1:T(8,128)} fusion(bf16[512,2048]{1,0:T(8,128)(2,1)} %all-gather.5.cloned.1.call-done, bf16[1,2048,684]{1,0,2:T(2,128)(2,1)} %get-tuple-element.13), kind=kOutput, calls=%fused_computation.27 | convolution fusion | flops 1434451968 | bytes 6299648 | tf_op jit(solution)/shard_map/dot_general | solution.py:35
  481.7 0.0 copy-done.5
  481.7 10.9 %fusion.24 = f32[512,2048]{1,0:T(8,128)} fusion(bf16[1,684,2048]{2,0,1:T(2,128)(2,1)} %get-tuple-element.17, bf16[512,2048]{1,0:T(8,128)(2,1)S(1)} %copy-done.5, bf16[1,2048,684]{1,0,2:T(2,128)(2,1)} %get-tuple-element.15, f32[512,684]{0,1:T(8,128)} %fusion.26), kind=kOutput, calls=%fused_computation.23 | convolution fusion | flops 2871005184 | bytes 13295616 | tf_op jit(solution)/shard_map/dot_general | solution.py:38
  492.6 0.0 reduce-scatter.5.cloned.1.call-update
  492.6 40.2 %reduce-scatter.5.cloned.1.call-done = f32[128,2048]{1,0:T(8,128)} async-done(((f32[512,2048]{1,0:T(8,128)}), f32[128,2048]{1,0:T(8,128)}) %reduce-scatter.5.cloned.1.call-update) | async-done | bytes 1048592 | tf_op jit(solution)/shard_map/reduce_scatter | solution.py:39
  532.9 41.2 %all-reduce.7 = bf16[128,2048]{1,0:T(8,128)(2,1)S(1)} all-reduce(f32[128,2048]{1,0:T(8,128)} %reduce-scatter.5.cloned.1.call-done), channel_id=1, replica_groups=mesh['tp'=4,'dp'=4] {'tp'}, use_global_device_ids=true, to_apply=%region_13.14 | all-reduce | flops 262144 | bytes 1572864 | tf_op jit(solution)/shard_map/psum | solution.py:40
  574.1 0.9 add.91
  (6 shorter events, 0.0 us)
Async XLA Ops:
  6.5 244.8 %all-gather.3.cloned.1.call-start = ((), (), s32[]{:S(2)}) async-start(), calls=%async_computation.2 | async-start | bytes 2621440 | tf_op jit(solution)/shard_map/all_gather | solution.py:34
  9.1 6.4 %copy-start.3 = (s32[128]{0:T(128)S(1)}, s32[128]{0:T(128)}, u32[]{:S(2)}) copy-start(s32[128]{0:T(128)} %param.11) | copy-start | bytes 1540
  163.9 47.5 %copy-start = (bf16[128,2048]{1,0:T(8,128)(2,1)S(1)}, bf16[128,2048]{1,0:T(8,128)(2,1)}, u32[]{:S(2)}) copy-start(bf16[128,2048]{1,0:T(8,128)(2,1)} %param.10) | copy-start | bytes 1572868
  163.9 47.8 %copy-start.1 = (bf16[2,2048]{1,0:T(2,128)(2,1)S(1)}, bf16[2,2048]{1,0:T(2,128)(2,1)}, u32[]{:S(2)}) copy-start(bf16[2,2048]{1,0:T(2,128)(2,1)} %param.14) | copy-start | bytes 24580
  212.7 96.7 %reduce-scatter.3.cloned.1.call-start = ((), (), s32[]{:S(2)}) async-start(), calls=%async_computation.3 | async-start | bytes 5242880 | tf_op jit(solution)/shard_map/reduce_scatter | solution.py:39
  213.0 29.2 %slice-start = ((s8[5603328]{0:T(1024)(128)(4,1)}), s8[4194304]{0:T(1024)(128)(4,1)S(1)}, s32[]{:S(2)}) async-start(s8[5603328]{0:T(1024)(128)(4,1)} %bitcast.74), calls=%async_computation.6 | async-start | bytes 8388608
  227.5 14.7 %slice-start.1 = ((s8[5603328]{0:T(1024)(128)(4,1)}), s8[1409024]{0:T(1024)(128)(4,1)S(1)}, s32[]{:S(2)}) async-start(s8[5603328]{0:T(1024)(128)(4,1)} %bitcast.74), calls=%async_computation.7 | async-start | bytes 2818048
  251.3 6.4 %copy-start.4 = (bf16[512,2048]{1,0:T(8,128)(2,1)S(1)}, bf16[512,2048]{1,0:T(8,128)(2,1)}, u32[]{:S(2)}) copy-start(bf16[512,2048]{1,0:T(8,128)(2,1)} %all-gather.3.cloned.1.call-done) | copy-start | bytes 6291460
  268.6 82.6 %copy-start.2 = (f32[1,2048]{1,0:T(1,128)S(1)}, f32[1,2048]{1,0:T(1,128)}, u32[]{:S(2)}) copy-start(f32[1,2048]{1,0:T(1,128)} %get-tuple-element.21) | copy-start | bytes 24580
  268.6 206.7 %all-gather.5.cloned.1.call-start = ((), (), s32[]{:S(2)}) async-start(), calls=%async_computation.4 | async-start | bytes 2621440 | tf_op jit(solution)/shard_map/all_gather | solution.py:34
  455.6 77.2 %reduce-scatter.5.cloned.1.call-start = ((), (), s32[]{:S(2)}) async-start(), calls=%async_computation.5 | async-start | bytes 5242880 | tf_op jit(solution)/shard_map/reduce_scatter | solution.py:39
  475.3 6.4 %copy-start.5 = (bf16[512,2048]{1,0:T(8,128)(2,1)S(1)}, bf16[512,2048]{1,0:T(8,128)(2,1)}, u32[]{:S(2)}) copy-start(bf16[512,2048]{1,0:T(8,128)(2,1)} %all-gather.5.cloned.1.call-done) | copy-start | bytes 6291460
Sparse Core Ops, SparseCore 0:
  212.8 20.9 all-gather.2
  268.7 40.6 reduce-scatter.2
  455.7 19.5 all-gather.4
  492.7 40.0 reduce-scatter.4
where the time goes:
time: 582 us
  blocking collectives  166 us (29%)
  matrix products  156 us (27%)
  local copies, waits for them, and re-layouts  138 us (24%)
  waiting for transfers between devices  100 us (17%)
  between operations  13.4 us (2%)
  other arithmetic  6.48 us (1%)
    squeeze x1, local copies, waits for them, and re-layouts, body(): c = cache[l]  97.1 us
    psum x2, blocking collectives, body(): attn = lax.psum(jnp.dot(o, wo[l], preferred_element_type=jnp.float32), 'tp')  83.8 us
    psum x2, blocking collectives, body(): y = lax.psum(y, 'tp')  82.6 us
    reduce_scatter x2, waiting for transfers between devices, body(): y = lax.psum_scatter(yp, 'dp', scatter_dimension=0, tiled=True)  81 us
    dot_general x2, matrix products, body(): jnp.einsum('bht,btk->bhk', p, c[:, :, :LAT], preferred_element_type=jnp.f...  51 us
    sub x2, matrix products, body(): jax.nn.softmax(jnp.where(keep, s, -jnp.inf), axis=-1).astype(jnp.bfloat16)  51 us
    dot_general x2, matrix products, body(): yp = jnp.dot(a, w2[l], preferred_element_type=jnp.float32)  21.8 us
    all_gather x2, waiting for transfers between devices, body(): gg = lax.all_gather(g, 'dp', axis=0, tiled=True)  19.4 us
  transfers between devices with their start and end apart: 4, of which 3 were waited for; matrix products, arithmetic and copies ran while one was open for 7% of the time, Pallas kernels for 0%

commit v1 on v0

v1 whole, which is shorter than its diff:
```python
import functools

import jax
import jax.numpy as jnp
from jax import lax
from jax.experimental import pallas as pl
from jax.experimental.pallas import tpu as pltpu
from jax.sharding import PartitionSpec as P

MESH = pl.DeviceIdType.MESH
F32 = jnp.float32
BF16 = jnp.bfloat16
LAT = 512
EPS = 1e-6
SCALE = 192 ** -0.5
VMEM_LIMIT = 64 * 1024 * 1024 - 65536 - 1024 * 1024

TP_ORDERS = (('z', 'y'), ('y', 'z'), ('z', 'y'), ('y', 'z'))
CUBE_ORDERS = (
    ('x', 'y', 'z'), ('y', 'z', 'x'), ('z', 'x', 'y'),
    ('x', 'y', 'z'), ('y', 'z', 'x'), ('z', 'x', 'y'),
    ('x', 'y', 'z'), ('y', 'z', 'x'),
)
RING = ((1, 0, 0), (0, 1, 0), (0, 0, 1), (0, 1, 1), (1, 1, 0), (1, 0, 1), (1, 1, 1))
TP_PEERS = ((1, 0), (0, 1), (1, 1))


class Place:
    def __init__(self):
        self.tp, self.dp = lax.axis_index('tp'), lax.axis_index('dp')
        self.z, self.y = lax.div(self.tp, 2), lax.rem(self.tp, 2)
        self.x, self.c = lax.div(self.dp, 2), lax.rem(self.dp, 2)
        self.at = {'x': self.x, 'z': self.z, 'y': self.y}

    def other(self, dx=0, dz=0, dy=0, dc=0):
        x = 1 - self.x if dx else self.x
        z = 1 - self.z if dz else self.z
        y = 1 - self.y if dy else self.y
        c = 1 - self.c if dc else self.c
        return {'tp': 2 * z + y, 'dp': 2 * x + c}

    def along(self, axis):
        return self.other(**{'d' + axis: 1})


def _send(src, dst, sems, k, device):
    copy = pltpu.make_async_remote_copy(
        src_ref=src, dst_ref=dst, send_sem=sems.at[0, k], recv_sem=sems.at[1, k],
        device_id=device, device_id_type=MESH,
    )
    copy.start()
    return copy


def _norm(v, w):
    vf = v.astype(F32)
    r = lax.rsqrt(jnp.mean(vf * vf, axis=-1, keepdims=True) + EPS)
    return (vf * r * w.astype(F32)).astype(BF16)


def _greet(devices):
    barrier = pltpu.get_barrier_semaphore()
    for device in devices:
        pl.semaphore_signal(barrier, inc=1, device_id=device, device_id_type=MESH)
    pl.semaphore_wait(barrier, len(devices))


class Halving:
    def __init__(self, here, axes, buf, recvs, sems, orders):
        self.here, self.axes, self.buf, self.recvs, self.sems, self.orders = here, axes, buf, recvs, sems, orders
        self.copies = {}

    def _view(self, chunk, phase, flip):
        index = [slice(None)] * len(self.axes)
        for p, axis in enumerate(self.orders[chunk][: phase + 1]):
            mine = self.here.at[axis]
            index[self.axes.index(axis)] = 1 - mine if (flip and p == phase) else mine
        return (chunk, *index)

    def send(self, chunk, phase):
        axis = self.orders[chunk][phase]
        self.copies[chunk, phase] = _send(
            self.buf.at[self._view(chunk, phase, True)], self.recvs[phase].at[chunk],
            self.sems, phase * len(self.orders) + chunk, self.here.along(axis),
        )

    def add(self, chunk, phase):
        self.copies[chunk, phase].wait_recv()
        view = self._view(chunk, phase, False)
        total = self.buf[view] + self.recvs[phase][chunk]
        if phase + 1 < len(self.axes):
            self.buf[view] = total
        return total

    def finish(self):
        for copy in self.copies.values():
            copy.wait_send()


def _q_exchange(here, h, wq_buf, wq_copies, q_send, q_recv, q_out, sems, width=768):
    copies = []
    cols = q_send.shape[-1]
    for n in range(cols // width):
        wq_copies[n].wait()
        part = slice(n * width, (n + 1) * width)
        q = jnp.dot(h, wq_buf[:, part], preferred_element_type=F32).astype(BF16)
        q_send[:, :, part] = q.reshape(4, -1, width)
        for k, (dz, dy) in enumerate(TP_PEERS):
            peer = here.other(dz=dz, dy=dy)
            copies.append(_send(
                q_send.at[peer['tp'], :, part], q_recv.at[here.tp, :, part], sems, 3 * n + k, peer,
            ))
    q_out[here.tp] = q_send[here.tp]
    for copy in copies:
        copy.wait_recv()
    for dz, dy in TP_PEERS:
        peer = here.other(dz=dz, dy=dy)
        q_out[peer['tp']] = q_recv[peer['tp']]
    for copy in copies:
        copy.wait_send()


def _wq_start(layer, wq_hbm, wq_buf, sems, width=768):
    copies = []
    for n in range(wq_buf.shape[1] // width):
        part = slice(n * width, (n + 1) * width)
        copies.append(pltpu.make_async_copy(wq_hbm.at[layer, :, part], wq_buf.at[:, part], sems.at[n]))
        copies[-1].start()
    return copies


def _first_kernel(x_ref, an_ref, wq_hbm, q_out, wq_buf, q_send, q_recv, wq_sems, q_sems):
    here = Place()
    wq_copies = _wq_start(0, wq_hbm, wq_buf, wq_sems)
    _greet([here.other(dz=dz, dy=dy) for dz, dy in TP_PEERS])
    h = _norm(x_ref[...], an_ref[0:1, :])
    _q_exchange(here, h, wq_buf, wq_copies, q_send, q_recv, q_out, q_sems)


def _attention_kernel(layer, len_ref, q_ref, cache_hbm, o_ref, c_buf, sems):
    depth, s_len, kv = c_buf.shape
    rows = q_ref.shape[0]
    block = 128
    blocks = s_len // block
    base = lax.axis_index('tp') * rows

    def length(b):
        return len_ref[base + b]

    def count(b):
        return lax.div(length(b) + (block - 1), block)

    def copy(b, j):
        slot = lax.rem(b, depth)
        part = pl.ds(j * block, block)
        return pltpu.make_async_copy(
            cache_hbm.at[layer, base + b, part, :], c_buf.at[slot, part, :], sems.at[slot, j]
        )

    def each(b, act):
        n = count(b)
        for j in range(blocks):
            @pl.when(j < n)
            def _():
                act(copy(b, j))

    c_buf[...] = jnp.zeros_like(c_buf)
    for b in range(depth - 2):
        each(b, lambda c: c.start())

    def attend(b, t):
        slot = lax.rem(b, depth)
        q = q_ref[b]
        s = lax.dot_general(
            q, c_buf[slot, 0:t, :], (((1,), (1,)), ((), ())), preferred_element_type=F32
        ) * SCALE
        keep = lax.broadcasted_iota(jnp.int32, s.shape, 1) < length(b)
        s = jnp.where(keep, s, -jnp.inf)
        e = jnp.exp(s - jnp.max(s, axis=-1, keepdims=True))
        p = (e / jnp.sum(e, axis=-1, keepdims=True)).astype(BF16)
        o = jnp.dot(p, c_buf[slot, 0:t, 0:LAT], preferred_element_type=F32)
        o_ref[b] = o.astype(BF16)

    @pl.loop(0, rows // 2)
    def _(i):
        b = 2 * i
        for k in range(2):
            @pl.when(b + depth - 2 + k < rows)
            def _():
                each(b + depth - 2 + k, lambda c: c.start())
        for k in range(2):
            each(b + k, lambda c: c.wait())
        n = jnp.maximum(count(b), count(b + 1))
        for m in range(1, blocks + 1):
            @pl.when(n == m)
            def _():
                attend(b, m * block)
                attend(b + 1, m * block)


def _layer_kernel(layer, last, o_ref, x_ref, an_ref, fn_ref, wo_hbm, w1_hbm, w3_hbm, w2_hbm, wq_hbm, *rest):
    outs, scratch = rest[: 1 if last else 2], rest[1 if last else 2:]
    (wo_buf, w1_buf, w3_buf, w2_buf, o_all, p_buf, pr1, pr2, g_all, a_buf, y_buf, yr1, yr2, yr3, x_buf, h_all,
     w_sems, ws_sems, o_sems, p_sems, g_sems, y_sems, h_sems, *more) = scratch
    here = Place()
    wo_copy = pltpu.make_async_copy(wo_hbm.at[layer], wo_buf, w_sems.at[0])
    wo_copy.start()
    own = [
        pltpu.make_async_copy(hbm.at[layer], buf.at[here.c], w_sems.at[1 + k])
        for k, (hbm, buf) in enumerate(((w3_hbm, w3_buf), (w1_hbm, w1_buf), (w2_hbm, w2_buf)))
    ]
    cube = [here.other(dx=dx, dz=dz, dy=dy) for dx, dz, dy in RING]
    partner = here.other(dc=1)
    _greet(cube + [partner])

    o_copies = []
    for k, (dz, dy) in enumerate(TP_PEERS):
        peer = here.other(dz=dz, dy=dy)
        o_copies.append(_send(o_ref.at[peer['tp']], o_all.at[here.tp], o_sems, k, peer))
    for copy in own:
        copy.start()
    swaps = [
        _send(hbm.at[layer], buf.at[here.c], ws_sems, k, partner)
        for k, (hbm, buf) in enumerate(((w3_hbm, w3_buf), (w1_hbm, w1_buf), (w2_hbm, w2_buf)))
    ]
    if not last:
        wq_buf, q_send, q_recv, wq_sems, q_sems = more
        wq_copies = _wq_start(layer + 1, wq_hbm, wq_buf, wq_sems)
    o_all[here.tp] = o_ref[here.tp]
    for copy in o_copies:
        copy.wait_recv()
    wo_copy.wait()

    heads, width = o_all.shape[1], p_buf.shape[-1]
    lhs = jnp.concatenate([o_all[:, h].reshape(-1, LAT) for h in range(heads)], axis=1)
    attn = Halving(here, ('z', 'y'), p_buf, (pr1, pr2), p_sems, TP_ORDERS)
    for n in range(len(TP_ORDERS)):
        part = slice(n * width, (n + 1) * width)
        p_buf[n] = jnp.dot(lhs, wo_buf[:, part], preferred_element_type=F32).reshape(p_buf.shape[1:])
        attn.send(n, 0)
    for n in range(len(TP_ORDERS)):
        attn.add(n, 0)
        attn.send(n, 1)
    x_mine = x_ref[here.tp] if layer == 0 else x_ref[...]
    for n in range(len(TP_ORDERS)):
        part = slice(n * width, (n + 1) * width)
        total = attn.add(n, 1).astype(BF16)
        x_buf[:, part] = (x_mine[:, part].astype(F32) + total.astype(F32)).astype(BF16)
    x_mid = x_buf[...]

    g_all[here.x, here.tp] = _norm(x_mid, fn_ref[layer:layer + 1, :])
    mine = g_all.at[here.x, here.tp]
    g_copies = [_send(mine, mine, g_sems, k, device) for k, device in enumerate(cube)]
    for copy in own:
        copy.wait()
    for copy in swaps:
        copy.wait_recv()
    for copy in g_copies:
        copy.wait_recv()

    g = g_all[...].reshape(-1, g_all.shape[-1])
    cols = w1_buf.shape[-1]

    @pl.loop(0, 2)
    def _(s):
        for lo in range(0, cols, 256):
            part = slice(lo, min(lo + 256, cols))
            u = jnp.dot(g, w3_buf[s, :, part], preferred_element_type=F32)
            v = jnp.dot(g, w1_buf[s, :, part], preferred_element_type=F32)
            a_buf[s, :, part] = (u * jax.nn.sigmoid(u) * v).astype(BF16)

    ffn = Halving(here, ('x', 'z', 'y'), y_buf, (yr1, yr2, yr3), y_sems, CUBE_ORDERS)
    width = y_buf.shape[-1]
    for n in range(len(CUBE_ORDERS)):
        part = slice(n * width, (n + 1) * width)
        y = jnp.dot(a_buf[0], w2_buf[0, :, part], preferred_element_type=F32)
        y += jnp.dot(a_buf[1], w2_buf[1, :, part], preferred_element_type=F32)
        y_buf[n] = y.reshape(y_buf.shape[1:])
        ffn.send(n, 0)
    for phase in range(2):
        for n in range(len(CUBE_ORDERS)):
            ffn.add(n, phase)
            ffn.send(n, phase + 1)
    for n in range(len(CUBE_ORDERS)):
        part = slice(n * width, (n + 1) * width)
        total = ffn.add(n, 2).astype(BF16)
        x_buf[:, part] = (x_mid[:, part].astype(F32) + total.astype(F32)).astype(BF16)
    x_new = x_buf[...]

    h_all[here.tp] = x_new if last else _norm(x_new, an_ref[layer + 1:layer + 2, :])
    mine = h_all.at[here.tp]
    h_copies = [
        _send(mine, mine, h_sems, k, here.other(dz=dz, dy=dy)) for k, (dz, dy) in enumerate(TP_PEERS)
    ]
    for copy in h_copies:
        copy.wait_recv()
    if last:
        outs[0][...] = h_all[...]
    else:
        outs[1][...] = x_new
        h = h_all[...].reshape(-1, h_all.shape[-1])
        _q_exchange(here, h, wq_buf, wq_copies, q_send, q_recv, outs[0], q_sems)
    attn.finish()
    ffn.finish()
    for copy in o_copies + swaps + g_copies + h_copies:
        copy.wait_send()


VM = pl.BlockSpec(memory_space=pltpu.VMEM)
ANY = pl.BlockSpec(memory_space=pl.ANY)
DMA = pltpu.SemaphoreType.DMA


def solution(mesh):
    def body(x, lengths, cache, attn_norm, ffn_norm, wq, wo, w1, w3, w2):
        nb, d = x.shape
        n_layers, _, s_len, kv = cache.shape
        heads = wq.shape[2] // kv
        rows = nb // 4
        cols = w1.shape[2]
        q_shape = (4, rows, heads * kv)

        def params(cid):
            return pltpu.CompilerParams(collective_id=cid, has_side_effects=True, vmem_limit_bytes=VMEM_LIMIT)

        q_scratch = [
            pltpu.VMEM((d, heads * kv), BF16),
            pltpu.VMEM(q_shape, BF16),
            pltpu.VMEM(q_shape, BF16),
            DMA((3,)),
            DMA((2, 9)),
        ]

        q = pl.pallas_call(
            _first_kernel,
            out_shape=jax.ShapeDtypeStruct(q_shape, BF16),
            in_specs=[VM, VM, ANY],
            out_specs=VM,
            scratch_shapes=q_scratch,
            compiler_params=params(0),
            name='q_first',
        )(x, attn_norm, wq)

        x_in = x.reshape(4, rows, d)
        for layer in range(n_layers):
            last = layer == n_layers - 1
            qt = q.reshape(4, rows, heads, kv).transpose(1, 0, 2, 3).reshape(rows, 4 * heads, kv)
            o = pl.pallas_call(
                functools.partial(_attention_kernel, layer),
                out_shape=jax.ShapeDtypeStruct((rows, 4 * heads, LAT), BF16),
                in_specs=[pl.BlockSpec(memory_space=pltpu.SMEM), VM, ANY],
                out_specs=VM,
                scratch_shapes=[pltpu.VMEM((8, s_len, kv), BF16), DMA((8, s_len // 128))],
                compiler_params=pltpu.CompilerParams(vmem_limit_bytes=VMEM_LIMIT),
                name='attention',
            )(lengths, qt, cache)
            ot = o.reshape(rows, 4, heads, LAT).transpose(1, 2, 0, 3)
            scratch = [
                pltpu.VMEM(wo.shape[1:], BF16),
                pltpu.VMEM((2, d, cols), BF16),
                pltpu.VMEM((2, d, cols), BF16),
                pltpu.VMEM((2, cols, d), BF16),
                pltpu.VMEM((4, heads, rows, LAT), BF16),
                pltpu.VMEM((4, 2, 2, rows, d // 4), F32),
                pltpu.VMEM((4, 2, rows, d // 4), F32),
                pltpu.VMEM((4, rows, d // 4), F32),
                pltpu.VMEM((2, 4, rows, d), BF16),
                pltpu.VMEM((2, 8 * rows, cols), BF16),
                pltpu.VMEM((8, 2, 2, 2, rows, d // 8), F32),
                pltpu.VMEM((8, 2, 2, rows, d // 8), F32),
                pltpu.VMEM((8, 2, rows, d // 8), F32),
                pltpu.VMEM((8, rows, d // 8), F32),
                pltpu.VMEM((rows, d), BF16),
                pltpu.VMEM((4, rows, d), BF16),
                DMA((4,)),
                DMA((2, 3)),
                DMA((2, 3)),
                DMA((2, 8)),
                DMA((2, 7)),
                DMA((2, 24)),
                DMA((2, 3)),
            ]
            if last:
                out_shape = [jax.ShapeDtypeStruct((4, rows, d), BF16)]
            else:
                out_shape = [jax.ShapeDtypeStruct(q_shape, BF16), jax.ShapeDtypeStruct((rows, d), BF16)]
                scratch += q_scratch
            outs = pl.pallas_call(
                functools.partial(_layer_kernel, layer, last),
                out_shape=out_shape,
                in_specs=[VM, VM, VM, VM, ANY, ANY, ANY, ANY, ANY],
                out_specs=[VM] * len(out_shape),
                scratch_shapes=scratch,
                compiler_params=params(1 + layer),
                name=f'layer_{layer}',
            )(ot, x_in, attn_norm, ffn_norm, wo, w1, w3, w2, wq)
            if last:
                return outs[0].reshape(nb, d)
            q, x_in = outs

    in_specs = (
        P('dp', None),
        P('dp'),
        P(None, 'dp', None, None),
        P(None, None),
        P(None, None),
        P(None, None, 'tp'),
        P(None, 'tp', None),
        P(None, None, ('dp', 'tp')),
        P(None, None, ('dp', 'tp')),
        P(None, ('dp', 'tp'), None),
    )
    return jax.shard_map(body, mesh=mesh, in_specs=in_specs, out_specs=P('dp', None), check_vma=False)
```

time: 582 us -> 450 us (0.77)
  Pallas kernels: 0 us -> 193 us
  blocking collectives: 166 us -> 0 us
  matrix products: 156 us -> 0 us
  local copies, waits for them, and re-layouts: 138 us -> 251 us
  waiting for transfers between devices: 100 us -> 0 us
  between operations: 13.4 us -> 0.08 us
  other arithmetic: 6.48 us -> 0 us
    unnamed x18 -> x5, local copies, waits for them, and re-layouts: 0.24 us -> 240 us
    pallas_call x0 -> x5, Pallas kernels: none -> 193 us  [the longest x2 135 us: body(): pl.pallas_call(functools.partial(_layer_kernel, layer, last), out_shape=o...]
    psum x4 -> x0, blocking collectives: 166 us -> none  [the longest x2 83.8 us: body(): attn = lax.psum(jnp.dot(o, wo[l], preferred_element_type=jnp.float32), 'tp')]
    dot_general x10 -> x0, matrix products: 105 us -> none  [the longest x2 51 us: body(): jnp.einsum('bht,btk->bhk', p, c[:, :, :LAT], preferred_element_type=jnp.f...]
    squeeze x1 -> x0, local copies, waits for them, and re-layouts: 97.1 us -> none  [body(): c = cache[l]]
    reduce_scatter x2 -> x0, waiting for transfers between devices: 81 us -> none  [body(): y = lax.psum_scatter(yp, 'dp', scatter_dimension=0, tiled=True)]
    sub x2 -> x0, matrix products: 51 us -> none  [body(): jax.nn.softmax(jnp.where(keep, s, -jnp.inf), axis=-1).astype(jnp.bfloat16)]
    slice x3 -> x0, local copies, waits for them, and re-layouts: 38.3 us -> none  [the longest x1 14.7 us: body(): v = jnp.dot(gg, w1[l], preferred_element_type=jnp.float32)]
  transfers between devices with their start and end apart: 4 -> 0, of which waited for: 3 -> 0; matrix products, arithmetic and copies ran while one was open for 7% -> 0% of each run, Pallas kernels for 0% -> 0%
where the time goes in v1:
time: 450 us; the launch traced here: 445 us
  local copies, waits for them, and re-layouts  251 us (56%)
  Pallas kernels  193 us (43%)
    unnamed x5, local copies, waits for them, and re-layouts  240 us
    pallas_call x2, Pallas kernels, body(): pl.pallas_call(functools.partial(_layer_kernel, layer, last), out_shape=o...  135 us
    pallas_call x2, Pallas kernels, body(): pl.pallas_call(functools.partial(_attention_kernel, layer), out_shape=jax...  42.4 us
    pallas_call x1, Pallas kernels, body(): pl.pallas_call(_first_kernel, out_shape=jax.ShapeDtypeStruct(q_shape, BF1...  15.8 us

profile of v1, /device:TPU:0, one launch (start us, length us, event | category | flops | bytes accessed | tf_op | source)
XLA Modules:
  0.0 444.7 jit_solution(7674370064062420196)
XLA Ops:
  0.0 15.8 %q_first.1 = bf16[4,32,2304]{2,1,0:T(8,128)(2,1)} custom-call(bf16[128,2048]{1,0:T(8,128)(2,1)} %x_ref.1, bf16[2,2048]{1,0:T(2,128)(2,1)} %an_ref.5, bf16[2,2048,2304]{2,1,0:T(8,128)(2,1)} %wq_hbm.5), custom_call_target="tpu_custom_call" | custom-call | tf_op jit(solution)/shard_map/q_first/pallas_call | solution.py:334
  15.8 2.1 reshape.24
  18.0 0.2 copy.26
  18.2 1.2 reshape.25.q_ref
  19.4 7.6 %copy.16.w2_hbm = bf16[2,684,2048]{2,1,0:T(8,128)(2,1)} copy(bf16[2,684,2048]{2,0,1:T(2,128)(2,1)} %param.19) | data formatting | bytes 11206656 | tf_op args[9]
  27.0 16.0 %copy.14.w1_hbm = bf16[2,2048,684]{2,1,0:T(8,128)(2,1)} copy(bf16[2,2048,684]{1,0,2:T(2,128)(2,1)} %param.17) | data formatting | bytes 11206656 | tf_op args[7]
  43.0 16.0 %copy.15.w3_hbm = bf16[2,2048,684]{2,1,0:T(8,128)(2,1)} copy(bf16[2,2048,684]{1,0,2:T(2,128)(2,1)} %param.18) | data formatting | bytes 11206656 | tf_op args[8]
  59.1 198.5 %copy.12.cache_hbm = bf16[2,128,512,576]{3,2,1,0:T(8,128)(2,1)} copy(bf16[2,128,512,576]{2,3,1,0:T(8,128)(2,1)} %param.12) | data formatting | bytes 301989888 | tf_op args[2]
  257.6 21.2 %attention.2 = bf16[32,16,512]{2,1,0:T(8,128)(2,1)} custom-call(s32[128]{0:T(128)} %len_ref.3, bf16[32,16,576]{2,1,0:T(8,128)(2,1)} %reshape.25.q_ref, bf16[2,128,512,576]{3,2,1,0:T(8,128)(2,1)} %copy.12.cache_hbm), custom_call_target="tpu_custom_call" | custom-call | tf_op jit(solution)/shard_map/attention/pallas_call | solution.py:348
  278.8 2.1 copy.13
  281.0 73.1 %layer_0.1 = (bf16[4,32,2304]{2,1,0:T(8,128)(2,1)}, bf16[32,2048]{1,0:T(8,128)(2,1)}) custom-call(bf16[4,4,32,512]{3,2,1,0:T(8,128)(2,1)} %bitcast.19, bf16[4,32,2048]{2,1,0:T(8,128)(2,1)} %bitcast.16, bf16[2,2048]{1,0:T(2,128)(2,1)} %an_ref.5, bf16[2,2048]{1,0:T(2,128)(2,1)} %fn_ref.3, bf16[2,2048,2048]{2,1,0:T(8,128)(2,1)} %wo_hbm.3, ...), custom_call_target="tpu_custom_call" | custom-call | tf_op jit(solution)/shard_map/layer_0/pallas_call | solution.py:388
  354.1 2.1 reshape.28
  356.3 0.2 copy.25
  356.5 1.2 reshape.29.q_ref
  357.7 21.2 %attention.3 = bf16[32,16,512]{2,1,0:T(8,128)(2,1)} custom-call(s32[128]{0:T(128)} %len_ref.3, bf16[32,16,576]{2,1,0:T(8,128)(2,1)} %reshape.29.q_ref, bf16[2,128,512,576]{3,2,1,0:T(8,128)(2,1)} %copy.12.cache_hbm), custom_call_target="tpu_custom_call" | custom-call | tf_op jit(solution)/shard_map/attention/pallas_call | solution.py:348
  378.9 2.1 copy.19
  381.0 61.8 %layer_1.1 = bf16[4,32,2048]{2,1,0:T(8,128)(2,1)} custom-call(bf16[4,4,32,512]{3,2,1,0:T(8,128)(2,1)} %bitcast.17, bf16[32,2048]{1,0:T(8,128)(2,1)} %get-tuple-element.8.x_ref, bf16[2,2048]{1,0:T(2,128)(2,1)} %an_ref.5, bf16[2,2048]{1,0:T(2,128)(2,1)} %fn_ref.3, bf16[2,2048,2048]{2,1,0:T(8,128)(2,1)} %wo_hbm.3, bf16[2,2048,684]{2,1,0:T(8,128)(2,1)} %copy.14.w1_hbm, ...), custom_call_target="tpu_custom_call" | custom-call | tf_op jit(solution)/shard_map/layer_1/pallas_call | solution.py:388
  442.8 1.9 copy.28

commit v2 on v1

--- a/solution.py
+++ b/solution.py
@@ -138,7 +138,7 @@
 
 
 def _attention_kernel(layer, len_ref, q_ref, cache_hbm, o_ref, c_buf, sems):
-    depth, s_len, kv = c_buf.shape
+    depth, kv, s_len = c_buf.shape
     rows = q_ref.shape[0]
     block = 128
     blocks = s_len // block
@@ -154,7 +154,7 @@
         slot = lax.rem(b, depth)
         part = pl.ds(j * block, block)
         return pltpu.make_async_copy(
-            cache_hbm.at[layer, base + b, part, :], c_buf.at[slot, part, :], sems.at[slot, j]
+            cache_hbm.at[layer, base + b, :, part], c_buf.at[slot, :, part], sems.at[slot, j]
         )
 
     def each(b, act):
@@ -171,15 +171,15 @@
     def attend(b, t):
         slot = lax.rem(b, depth)
         q = q_ref[b]
-        s = lax.dot_general(
-            q, c_buf[slot, 0:t, :], (((1,), (1,)), ((), ())), preferred_element_type=F32
-        ) * SCALE
+        s = jnp.dot(q, c_buf[slot, :, 0:t], preferred_element_type=F32) * SCALE
         keep = lax.broadcasted_iota(jnp.int32, s.shape, 1) < length(b)
         s = jnp.where(keep, s, -jnp.inf)
         e = jnp.exp(s - jnp.max(s, axis=-1, keepdims=True))
         p = (e / jnp.sum(e, axis=-1, keepdims=True)).astype(BF16)
-        o = jnp.dot(p, c_buf[slot, 0:t, 0:LAT], preferred_element_type=F32)
-        o_ref[b] = o.astype(BF16)
+        o = lax.dot_general(
+            c_buf[slot, 0:LAT, 0:t], p, (((1,), (1,)), ((), ())), preferred_element_type=F32
+        )
+        o_ref[b] = o.T.astype(BF16)
 
     @pl.loop(0, rows // 2)
     def _(i):
@@ -259,15 +259,15 @@
         copy.wait_recv()
 
     g = g_all[...].reshape(-1, g_all.shape[-1])
-    cols = w1_buf.shape[-1]
+    cols = w1_buf.shape[1]
 
     @pl.loop(0, 2)
     def _(s):
         for lo in range(0, cols, 256):
             part = slice(lo, min(lo + 256, cols))
-            u = jnp.dot(g, w3_buf[s, :, part], preferred_element_type=F32)
-            v = jnp.dot(g, w1_buf[s, :, part], preferred_element_type=F32)
-            a_buf[s, :, part] = (u * jax.nn.sigmoid(u) * v).astype(BF16)
+            u = lax.dot_general(w3_buf[s, part, :], g, (((1,), (1,)), ((), ())), preferred_element_type=F32)
+            v = lax.dot_general(w1_buf[s, part, :], g, (((1,), (1,)), ((), ())), preferred_element_type=F32)
+            a_buf[s, :, part] = (u * jax.nn.sigmoid(u) * v).T.astype(BF16)
 
     ffn = Halving(here, ('x', 'z', 'y'), y_buf, (yr1, yr2, yr3), y_sems, CUBE_ORDERS)
     width = y_buf.shape[-1]
@@ -341,6 +341,8 @@
             name='q_first',
         )(x, attn_norm, wq)
 
+        cache_t = cache.transpose(0, 1, 3, 2)
+        w1_t, w3_t = w1.transpose(0, 2, 1), w3.transpose(0, 2, 1)
         x_in = x.reshape(4, rows, d)
         for layer in range(n_layers):
             last = layer == n_layers - 1
@@ -350,15 +352,15 @@
                 out_shape=jax.ShapeDtypeStruct((rows, 4 * heads, LAT), BF16),
                 in_specs=[pl.BlockSpec(memory_space=pltpu.SMEM), VM, ANY],
                 out_specs=VM,
-                scratch_shapes=[pltpu.VMEM((8, s_len, kv), BF16), DMA((8, s_len // 128))],
+                scratch_shapes=[pltpu.VMEM((8, kv, s_len), BF16), DMA((8, s_len // 128))],
                 compiler_params=pltpu.CompilerParams(vmem_limit_bytes=VMEM_LIMIT),
                 name='attention',
-            )(lengths, qt, cache)
+            )(lengths, qt, cache_t)
             ot = o.reshape(rows, 4, heads, LAT).transpose(1, 2, 0, 3)
             scratch = [
                 pltpu.VMEM(wo.shape[1:], BF16),
-                pltpu.VMEM((2, d, cols), BF16),
-                pltpu.VMEM((2, d, cols), BF16),
+                pltpu.VMEM((2, cols, d), BF16),
+                pltpu.VMEM((2, cols, d), BF16),
                 pltpu.VMEM((2, cols, d), BF16),
                 pltpu.VMEM((4, heads, rows, LAT), BF16),
                 pltpu.VMEM((4, 2, 2, rows, d // 4), F32),
@@ -393,7 +395,7 @@
                 scratch_shapes=scratch,
                 compiler_params=params(1 + layer),
                 name=f'layer_{layer}',
-            )(ot, x_in, attn_norm, ffn_norm, wo, w1, w3, w2, wq)
+            )(ot, x_in, attn_norm, ffn_norm, wo, w1_t, w3_t, w2, wq)
             if last:
                 return outs[0].reshape(nb, d)
             q, x_in = outs

time: 450 us -> 225 us (0.50); the launches traced: 445 us -> 225 us
  local copies, waits for them, and re-layouts: 251 us -> 34.6 us
    unnamed x5 -> x2, local copies, waits for them, and re-layouts: 240 us -> 9.45 us
    transpose x0 -> x1, local copies, waits for them, and re-layouts: none -> 13.8 us  [body(): w1_t, w3_t = (w1.transpose(0, 2, 1), w3.transpose(0, 2, 1))]
    pallas_call x2, Pallas kernels: 42.4 us -> 35 us  [body(): pl.pallas_call(functools.partial(_attention_kernel, layer), out_shape=jax...]
where the time goes in v2:
time: 225 us
  Pallas kernels  190 us (84%)
  local copies, waits for them, and re-layouts  34.6 us (15%)
    pallas_call x2, Pallas kernels, body(): pl.pallas_call(functools.partial(_layer_kernel, layer, last), out_shape=o...  139 us
    pallas_call x2, Pallas kernels, body(): pl.pallas_call(functools.partial(_attention_kernel, layer), out_shape=jax...  35 us
    pallas_call x1, Pallas kernels, body(): pl.pallas_call(_first_kernel, out_shape=jax.ShapeDtypeStruct(q_shape, BF1...  15.8 us
    transpose x1, local copies, waits for them, and re-layouts, body(): w1_t, w3_t = (w1.transpose(0, 2, 1), w3.transpose(0, 2, 1))  13.8 us
    unnamed x2, local copies, waits for them, and re-layouts  9.45 us
    reshape x6, local copies, waits for them, and re-layouts, body(): q.reshape(4, rows, heads, kv).transpose(1, 0, 2, 3)  7.08 us

profile of v2, /device:TPU:0, one launch (start us, length us, event | category | flops | bytes accessed | tf_op | source)
XLA Modules:
  0.0 224.7 jit_solution(12557955511334779148)
XLA Ops:
  0.0 15.8 %q_first.1 = bf16[4,32,2304]{2,1,0:T(8,128)(2,1)} custom-call(bf16[128,2048]{1,0:T(8,128)(2,1)} %x_ref.1, bf16[2,2048]{1,0:T(2,128)(2,1)} %an_ref.5, bf16[2,2048,2304]{2,1,0:T(8,128)(2,1)} %wq_hbm.5), custom_call_target="tpu_custom_call" | custom-call | tf_op jit(solution)/shard_map/q_first/pallas_call | solution.py:334
  15.8 2.1 reshape.24
  18.0 0.2 copy.24
  18.2 1.2 reshape.25.q_ref
  19.4 17.5 %attention.2 = bf16[32,16,512]{2,1,0:T(8,128)(2,1)} custom-call(s32[128]{0:T(128)} %len_ref.3, bf16[32,16,576]{2,1,0:T(8,128)(2,1)} %reshape.25.q_ref, bf16[2,128,576,512]{3,2,1,0:T(8,128)(2,1)} %bitcast.1.cache_hbm), custom_call_target="tpu_custom_call" | custom-call | tf_op jit(solution)/shard_map/attention/pallas_call | solution.py:350
  36.9 2.1 copy.12
  39.0 7.6 %copy.15.w2_hbm = bf16[2,684,2048]{2,1,0:T(8,128)(2,1)} copy(bf16[2,684,2048]{2,0,1:T(2,128)(2,1)} %param.19) | data formatting | bytes 11206656 | tf_op args[9]
  46.6 13.8 %copy_bitcast_fusion = (bf16[2,684,2048]{2,1,0:T(8,128)(2,1)}, bf16[2,684,2048]{2,1,0:T(8,128)(2,1)}) fusion(bf16[2,2048,684]{1,0,2:T(2,128)(2,1)} %param.18, bf16[2,2048,684]{1,0,2:T(2,128)(2,1)} %param.17), kind=kLoop, calls=%fused_computation | loop fusion | bytes 22413312 | tf_op jit(solution)/shard_map/transpose | solution.py:345
  60.4 73.5 %layer_0.1 = (bf16[4,32,2304]{2,1,0:T(8,128)(2,1)}, bf16[32,2048]{1,0:T(8,128)(2,1)}) custom-call(bf16[4,4,32,512]{3,2,1,0:T(8,128)(2,1)} %bitcast.22, bf16[4,32,2048]{2,1,0:T(8,128)(2,1)} %bitcast.21, bf16[2,2048]{1,0:T(2,128)(2,1)} %an_ref.5, bf16[2,2048]{1,0:T(2,128)(2,1)} %fn_ref.3, bf16[2,2048,2048]{2,1,0:T(8,128)(2,1)} %wo_hbm.3, ...), custom_call_target="tpu_custom_call" | custom-call | tf_op jit(solution)/shard_map/layer_0/pallas_call | solution.py:390
  134.0 2.1 reshape.28
  136.1 0.2 copy.23
  136.3 1.2 reshape.29.q_ref
  137.5 17.5 %attention.3 = bf16[32,16,512]{2,1,0:T(8,128)(2,1)} custom-call(s32[128]{0:T(128)} %len_ref.3, bf16[32,16,576]{2,1,0:T(8,128)(2,1)} %reshape.29.q_ref, bf16[2,128,576,512]{3,2,1,0:T(8,128)(2,1)} %bitcast.1.cache_hbm), custom_call_target="tpu_custom_call" | custom-call | tf_op jit(solution)/shard_map/attention/pallas_call | solution.py:350
  155.0 2.1 copy.17
  157.2 65.6 %layer_1.1 = bf16[4,32,2048]{2,1,0:T(8,128)(2,1)} custom-call(bf16[4,4,32,512]{3,2,1,0:T(8,128)(2,1)} %bitcast.23, bf16[32,2048]{1,0:T(8,128)(2,1)} %get-tuple-element.8.x_ref, bf16[2,2048]{1,0:T(2,128)(2,1)} %an_ref.5, bf16[2,2048]{1,0:T(2,128)(2,1)} %fn_ref.3, bf16[2,2048,2048]{2,1,0:T(8,128)(2,1)} %wo_hbm.3, ...), custom_call_target="tpu_custom_call" | custom-call | tf_op jit(solution)/shard_map/layer_1/pallas_call | solution.py:390
  222.8 1.9 copy.26

commit v3 on v0

v3 whole, which is shorter than its diff:
```python
import functools

import jax
import jax.numpy as jnp
from jax import lax
from jax.experimental import pallas as pl
from jax.experimental.pallas import tpu as pltpu
from jax.sharding import PartitionSpec as P

MESH = pl.DeviceIdType.MESH
F32 = jnp.float32
BF16 = jnp.bfloat16
LAT = 512
EPS = 1e-6
SCALE = 192 ** -0.5
VMEM_LIMIT = 64 * 1024 * 1024 - 65536

TP_ORDERS = (('z', 'y'), ('y', 'z'), ('z', 'y'), ('y', 'z'))
CUBE_ORDERS = (
    ('x', 'y', 'z'), ('y', 'z', 'x'), ('z', 'x', 'y'),
    ('x', 'y', 'z'), ('y', 'z', 'x'), ('z', 'x', 'y'),
    ('x', 'y', 'z'), ('y', 'z', 'x'),
)
RING = ((1, 0, 0), (0, 1, 0), (0, 0, 1), (0, 1, 1), (1, 1, 0), (1, 0, 1), (1, 1, 1))
TP_PEERS = ((1, 0), (0, 1), (1, 1))


class Place:
    def __init__(self):
        self.tp, self.dp = lax.axis_index('tp'), lax.axis_index('dp')
        self.z, self.y = lax.div(self.tp, 2), lax.rem(self.tp, 2)
        self.x, self.c = lax.div(self.dp, 2), lax.rem(self.dp, 2)
        self.at = {'x': self.x, 'z': self.z, 'y': self.y}

    def other(self, dx=0, dz=0, dy=0, dc=0):
        x = 1 - self.x if dx else self.x
        z = 1 - self.z if dz else self.z
        y = 1 - self.y if dy else self.y
        c = 1 - self.c if dc else self.c
        return {'tp': 2 * z + y, 'dp': 2 * x + c}

    def along(self, axis):
        return self.other(**{'d' + axis: 1})


def _send(src, dst, sems, k, device):
    copy = pltpu.make_async_remote_copy(
        src_ref=src, dst_ref=dst, send_sem=sems.at[0, k], recv_sem=sems.at[1, k],
        device_id=device, device_id_type=MESH,
    )
    copy.start()
    return copy


def _norm(v, w):
    vf = v.astype(F32)
    r = lax.rsqrt(jnp.mean(vf * vf, axis=-1, keepdims=True) + EPS)
    return (vf * r * w.astype(F32)).astype(BF16)


def _greet(devices):
    barrier = pltpu.get_barrier_semaphore()
    for device in devices:
        pl.semaphore_signal(barrier, inc=1, device_id=device, device_id_type=MESH)
    pl.semaphore_wait(barrier, len(devices))


class Halving:
    def __init__(self, here, axes, buf, recvs, sems, orders):
        self.here, self.axes, self.buf, self.recvs, self.sems, self.orders = here, axes, buf, recvs, sems, orders
        self.copies = {}

    def _view(self, chunk, phase, flip):
        index = [slice(None)] * len(self.axes)
        for p, axis in enumerate(self.orders[chunk][: phase + 1]):
            mine = self.here.at[axis]
            index[self.axes.index(axis)] = 1 - mine if (flip and p == phase) else mine
        return (chunk, *index)

    def send(self, chunk, phase):
        axis = self.orders[chunk][phase]
        self.copies[chunk, phase] = _send(
            self.buf.at[self._view(chunk, phase, True)], self.recvs[phase].at[chunk],
            self.sems, phase * len(self.orders) + chunk, self.here.along(axis),
        )

    def add(self, chunk, phase):
        self.copies[chunk, phase].wait_recv()
        view = self._view(chunk, phase, False)
        total = self.buf[view] + self.recvs[phase][chunk]
        if phase + 1 < len(self.axes):
            self.buf[view] = total
        return total

    def finish(self):
        for copy in self.copies.values():
            copy.wait_send()


def _kernel(
    len_ref, x_ref, an_ref, fn_ref, cache_hbm, wq_hbm, wo_hbm, w1_hbm, w3_hbm, w2_hbm, out_ref,
    wq_buf, wo_buf, w_buf, stage, c_buf, h_buf, q_send, q_recv, q_att, o_rows, o_send, o_all,
    p_buf, pr1, pr2, x_buf, g_all, g_buf, a_buf, y_buf, yr1, yr2, yr3, h_all,
    wq_sems, wo_sem, st_sems, ws_sems, c_sems, q_sems, o_sems, p_sems, g_sems, y_sems, h_sems, credit,
):
    here = Place()
    n_layers = cache_hbm.shape[0]
    d = x_buf.shape[1]
    rows = x_buf.shape[0]
    unit = c_buf.shape[1]
    units = rows // unit
    cols = w_buf.shape[2]
    chunk = stage.shape[1]
    heads = o_send.shape[2]
    kv = c_buf.shape[2]
    q_width = q_send.shape[-1] // 3
    partner = here.other(dc=1)
    peers = [here.other(dz=dz, dy=dy) for dz, dy in TP_PEERS]
    cube = [here.other(dx=dx, dz=dz, dy=dy) for dx, dz, dy in RING]

    def wq_copy(layer, n):
        part = slice(n * q_width, (n + 1) * q_width)
        return pltpu.make_async_copy(wq_hbm.at[layer, :, part], wq_buf.at[:, part], wq_sems.at[n])

    def wo_copy(layer):
        return pltpu.make_async_copy(wo_hbm.at[layer], wo_buf, wo_sem.at[0])

    def cache_copy(layer, i):
        slot = lax.rem(i, 2)
        return pltpu.make_async_copy(
            cache_hbm.at[layer, pl.ds(here.tp * rows + i * unit, unit)], c_buf.at[slot], c_sems.at[slot]
        )

    pieces = [
        (k, hbm, lo, min(chunk, cols - lo))
        for k, hbm in enumerate((w3_hbm, w1_hbm, w2_hbm)) for lo in range(0, cols, chunk)
    ]
    ring = stage.shape[0]

    def piece_copy(i):
        _, hbm, lo, n = pieces[i]
        return pltpu.make_async_copy(hbm.at[lo:lo + n], stage.at[i % ring, 0:n], st_sems.at[i % ring])

    def unpack(layer, i):
        k, _, lo, n = pieces[i]
        slot = i % ring

        @pl.loop(0, n // 16)
        def _(j):
            r = pl.multiple_of(j * 16, 16)
            pair = pltpu.einshape('alk->lak', stage[slot, pl.ds(r, 16)])
            w_buf[k, here.c, pl.ds(pl.multiple_of(lo + r, 16), 16), :] = pair[layer]
        if n % 16:
            r = n - n % 16
            pair = pltpu.einshape('alk->lak', stage[slot, r:n])
            w_buf[k, here.c, lo + r:lo + n, :] = pair[layer]

    for n in range(3):
        wq_copy(0, n).start()
    for i in range(2):
        cache_copy(0, i).start()
    for i in range(ring):
        piece_copy(i).start()
    wo_copy(0).start()
    _greet(cube + [partner])

    for layer in range(n_layers):
        last = layer + 1 == n_layers
        x_all = x_ref if layer == 0 else h_all

        for t in range(4):
            h_buf[t * rows:(t + 1) * rows, :] = _norm(x_all[t], an_ref[layer:layer + 1, :])
        q_copies = []
        for n in range(3):
            wq_copy(layer, n).wait()
            part = slice(n * q_width, (n + 1) * q_width)
            q = jnp.dot(h_buf[...], wq_buf[:, part], preferred_element_type=F32).astype(BF16)
            q_send[:, :, part] = q.reshape(4, rows, q_width)
            for k, peer in enumerate(peers):
                q_copies.append(_send(
                    q_send.at[peer['tp'], :, part], q_recv.at[here.tp, :, part], q_sems, 3 * n + k, peer,
                ))
        if not last:
            for n in range(3):
                wq_copy(layer + 1, n).start()
        q_recv[here.tp] = q_send[here.tp]

        swaps = []
        for i in range(len(pieces)):
            piece_copy(i).wait()
            unpack(layer, i)
            if i + ring < len(pieces):
                piece_copy(i + ring).start()
            k = pieces[i][0]
            if i + 1 == len(pieces) or pieces[i + 1][0] != k:
                if layer and k == 0:
                    pl.semaphore_wait(credit, 1)
                mine = w_buf.at[k, here.c]
                swaps.append(_send(mine, mine, ws_sems, k, partner))
        if not last:
            for i in range(ring):
                piece_copy(i).start()

        for copy in q_copies:
            copy.wait_recv()
        for h in range(heads):
            q = q_recv[:, :, h * kv:(h + 1) * kv]
            q_att[:, 4 * h:4 * h + 4, :] = pltpu.einshape('tbk->btk', q)

        def o_copy(i, k):
            return pltpu.make_async_remote_copy(
                src_ref=o_send.at[peers[k]['tp'], i], dst_ref=o_all.at[here.tp, i],
                send_sem=o_sems.at[0, 3 * i + k], recv_sem=o_sems.at[1, 3 * i + k],
                device_id=peers[k], device_id_type=MESH,
            )

        @pl.loop(0, units)
        def _(i):
            slot = lax.rem(i, 2)
            cache_copy(layer, i).wait()
            for lo in range(0, unit, 4):
                scores = [
                    jnp.dot(q_att[i * unit + k], c_buf[slot, k], preferred_element_type=F32)
                    for k in range(lo, lo + 4)
                ]
                probs = []
                for k, s in enumerate(scores, lo):
                    keep = lax.broadcasted_iota(jnp.int32, s.shape, 1) < len_ref[here.tp * rows + i * unit + k]
                    s = jnp.where(keep, s * SCALE, -jnp.inf)
                    e = jnp.exp(s - jnp.max(s, axis=-1, keepdims=True))
                    probs.append((e / jnp.sum(e, axis=-1, keepdims=True)).astype(BF16))
                for k, p in enumerate(probs, lo):
                    o = lax.dot_general(
                        p, c_buf[slot, k, 0:LAT, :], (((1,), (1,)), ((), ())), preferred_element_type=F32
                    )
                    for j in range(LAT // 128):
                        o_rows[j, k * 16:(k + 1) * 16, :] = o[:, j * 128:(j + 1) * 128]
            for h in range(heads):
                for t in range(4):
                    for j in range(LAT // 128):
                        part = slice(j * 128, (j + 1) * 128)
                        o_send[t, i, h, :, part] = o_rows[j, pl.ds(4 * h + t, unit, stride=16), :].astype(BF16)
            for k in range(3):
                o_copy(i, k).start()
            o_all[here.tp, i] = o_send[here.tp, i]

            @pl.when(i + 2 < units)
            def _():
                cache_copy(layer, i + 2).start()
        if not last:
            for i in range(2):
                cache_copy(layer + 1, i).start()
        wo_copy(layer).wait()
        for i in range(units):
            for k in range(3):
                o_copy(i, k).wait_recv()

        width = p_buf.shape[-1]
        lhs = jnp.concatenate([o_all[:, :, h].reshape(4 * rows, LAT) for h in range(heads)], axis=1)
        attn = Halving(here, ('z', 'y'), p_buf, (pr1, pr2), p_sems, TP_ORDERS)
        for n in range(len(TP_ORDERS)):
            part = slice(n * width, (n + 1) * width)
            p_buf[n] = jnp.dot(lhs, wo_buf[:, part], preferred_element_type=F32).reshape(p_buf.shape[1:])
            attn.send(n, 0)
        if not last:
            wo_copy(layer + 1).start()
        for n in range(len(TP_ORDERS)):
            attn.add(n, 0)
            attn.send(n, 1)
        x_mine = x_ref[here.tp] if layer == 0 else x_buf[...]
        g_copies = []
        for n in range(len(TP_ORDERS)):
            part = slice(n * width, (n + 1) * width)
            total = attn.add(n, 1).astype(BF16)
            x_part = (x_mine[:, part].astype(F32) + total.astype(F32)).astype(BF16)
            x_buf[:, part] = x_part
            g_all[here.x, here.tp, :, part] = x_part
            mine = g_all.at[here.x, here.tp, :, part]
            g_copies.append([_send(mine, mine, g_sems, 7 * n + k, device) for k, device in enumerate(cube)])

        def g_norm(x, t):
            at = pl.multiple_of((4 * x + t) * rows, rows)
            g_buf[pl.ds(at, rows), :] = _norm(g_all[x, t], fn_ref[layer:layer + 1, :])

        g_norm(here.x, here.tp)
        for copy in swaps:
            copy.wait_recv()
        for k, device in enumerate(cube):
            for copies in g_copies:
                copies[k].wait_recv()
            g_norm(lax.div(device['dp'], 2), device['tp'])

        @pl.loop(0, 2)
        def _(s):
            for lo in range(0, cols, 256):
                part = slice(lo, min(lo + 256, cols))
                u, v = (
                    lax.dot_general(
                        w_buf[k, s, part, :], g_buf[...], (((1,), (1,)), ((), ())), preferred_element_type=F32
                    ) for k in range(2)
                )
                a_buf[s, :, part] = (u * jax.nn.sigmoid(u) * v).T.astype(BF16)

        ffn = Halving(here, ('x', 'z', 'y'), y_buf, (yr1, yr2, yr3), y_sems, CUBE_ORDERS)
        width = y_buf.shape[-1]
        for n in range(len(CUBE_ORDERS)):
            part = slice(n * width, (n + 1) * width)
            y = jnp.dot(a_buf[0], w_buf[2, 0, :, part], preferred_element_type=F32)
            y += jnp.dot(a_buf[1], w_buf[2, 1, :, part], preferred_element_type=F32)
            y_buf[n] = y.reshape(y_buf.shape[1:])
            ffn.send(n, 0)
        if not last:
            pl.semaphore_signal(credit, inc=1, device_id=partner, device_id_type=MESH)
        for phase in range(2):
            for n in range(len(CUBE_ORDERS)):
                ffn.add(n, phase)
                ffn.send(n, phase + 1)
        h_copies = []
        for n in range(len(CUBE_ORDERS)):
            part = slice(n * width, (n + 1) * width)
            total = ffn.add(n, 2).astype(BF16)
            x_part = (x_buf[:, part].astype(F32) + total.astype(F32)).astype(BF16)
            x_buf[:, part] = x_part
            h_all[here.tp, :, part] = x_part
            mine = h_all.at[here.tp, :, part]
            h_copies += [_send(mine, mine, h_sems, 3 * n + k, peer) for k, peer in enumerate(peers)]

        for copy in h_copies:
            copy.wait_recv()
        attn.finish()
        ffn.finish()
        for copy in q_copies + swaps + h_copies + [copy for copies in g_copies for copy in copies]:
            copy.wait_send()
        for i in range(units):
            for k in range(3):
                o_copy(i, k).wait_send()
    out_ref[...] = h_all[...]


VM = pl.BlockSpec(memory_space=pltpu.VMEM)
SM = pl.BlockSpec(memory_space=pltpu.SMEM)
ANY = pl.BlockSpec(memory_space=pl.ANY)
DMA = pltpu.SemaphoreType.DMA


def solution(mesh):
    def body(x, lengths, cache, attn_norm, ffn_norm, wq, wo, w1, w3, w2):
        nb, d = x.shape
        s_len, kv = cache.shape[2:]
        heads = wq.shape[2] // kv
        rows = nb // 4
        cols = w1.shape[2]
        unit = 8
        q_shape = (4, rows, heads * kv)
        scratch = [
            pltpu.VMEM(wq.shape[1:], BF16),
            pltpu.VMEM(wo.shape[1:], BF16),
            pltpu.VMEM((3, 2, cols, d), BF16),
            pltpu.VMEM((2, 176, 2, d), BF16),
            pltpu.VMEM((2, unit, kv, s_len), BF16),
            pltpu.VMEM((nb, d), BF16),
            pltpu.VMEM(q_shape, BF16),
            pltpu.VMEM(q_shape, BF16),
            pltpu.VMEM((rows, 4 * heads, kv), BF16),
            pltpu.VMEM((LAT // 128, unit * 4 * heads, 128), F32),
            pltpu.VMEM((4, rows // unit, heads, unit, LAT), BF16),
            pltpu.VMEM((4, rows // unit, heads, unit, LAT), BF16),
            pltpu.VMEM((4, 2, 2, rows, d // 4), F32),
            pltpu.VMEM((4, 2, rows, d // 4), F32),
            pltpu.VMEM((4, rows, d // 4), F32),
            pltpu.VMEM((rows, d), BF16),
            pltpu.VMEM((2, 4, rows, d), BF16),
            pltpu.VMEM((8 * rows, d), BF16),
            pltpu.VMEM((2, 8 * rows, cols), BF16),
            pltpu.VMEM((8, 2, 2, 2, rows, d // 8), F32),
            pltpu.VMEM((8, 2, 2, rows, d // 8), F32),
            pltpu.VMEM((8, 2, rows, d // 8), F32),
            pltpu.VMEM((8, rows, d // 8), F32),
            pltpu.VMEM((4, rows, d), BF16),
            DMA((3,)),
            DMA((1,)),
            DMA((2,)),
            DMA((2, 3)),
            DMA((2,)),
            DMA((2, 9)),
            DMA((2, 12)),
            DMA((2, 8)),
            DMA((2, 28)),
            DMA((2, 24)),
            DMA((2, 24)),
            pltpu.SemaphoreType.REGULAR,
        ]
        out = pl.pallas_call(
            _kernel,
            out_shape=jax.ShapeDtypeStruct((4, rows, d), BF16),
            in_specs=[SM, VM, VM, VM] + [ANY] * 6,
            out_specs=VM,
            scratch_shapes=scratch,
            compiler_params=pltpu.CompilerParams(
                collective_id=0, has_side_effects=True, vmem_limit_bytes=VMEM_LIMIT,
            ),
            name='two_layers',
        )(
            lengths, x.reshape(4, rows, d), attn_norm, ffn_norm, cache.transpose(0, 1, 3, 2), wq, wo,
            w1.transpose(2, 0, 1), w3.transpose(2, 0, 1), w2.transpose(1, 0, 2),
        )
        return out.reshape(nb, d)

    in_specs = (
        P('dp', None),
        P('dp'),
        P(None, 'dp', None, None),
        P(None, None),
        P(None, None),
        P(None, None, 'tp'),
        P(None, 'tp', None),
        P(None, None, ('dp', 'tp')),
        P(None, None, ('dp', 'tp')),
        P(None, ('dp', 'tp'), None),
    )
    return jax.shard_map(body, mesh=mesh, in_specs=in_specs, out_specs=P('dp', None), check_vma=False)
```

time: 582 us -> 163 us (0.28)
  blocking collectives: 166 us -> 0 us
  Pallas kernels: 0 us -> 160 us
  matrix products: 156 us -> 0 us
  local copies, waits for them, and re-layouts: 138 us -> 1.88 us
  waiting for transfers between devices: 100 us -> 0 us
  between operations: 13.4 us -> 0.01 us
  other arithmetic: 6.48 us -> 0 us
    psum x4 -> x0, blocking collectives: 166 us -> none  [the longest x2 83.8 us: body(): attn = lax.psum(jnp.dot(o, wo[l], preferred_element_type=jnp.float32), 'tp')]
    pallas_call x0 -> x1, Pallas kernels: none -> 160 us  [body(): pl.pallas_call(_kernel, out_shape=jax.ShapeDtypeStruct((4, rows, d), BF16...]
    dot_general x10 -> x0, matrix products: 105 us -> none  [the longest x2 51 us: body(): jnp.einsum('bht,btk->bhk', p, c[:, :, :LAT], preferred_element_type=jnp.f...]
    squeeze x1 -> x0, local copies, waits for them, and re-layouts: 97.1 us -> none  [body(): c = cache[l]]
    reduce_scatter x2 -> x0, waiting for transfers between devices: 81 us -> none  [body(): y = lax.psum_scatter(yp, 'dp', scatter_dimension=0, tiled=True)]
    sub x2 -> x0, matrix products: 51 us -> none  [body(): jax.nn.softmax(jnp.where(keep, s, -jnp.inf), axis=-1).astype(jnp.bfloat16)]
    slice x3 -> x0, local copies, waits for them, and re-layouts: 38.3 us -> none  [the longest x1 14.7 us: body(): v = jnp.dot(gg, w1[l], preferred_element_type=jnp.float32)]
    all_gather x2 -> x0, waiting for transfers between devices: 19.4 us -> none  [body(): gg = lax.all_gather(g, 'dp', axis=0, tiled=True)]
  transfers between devices with their start and end apart: 4 -> 0, of which waited for: 3 -> 0; matrix products, arithmetic and copies ran while one was open for 7% -> 0% of each run, Pallas kernels for 0% -> 0%
where the time goes in v3:
time: 163 us; the launch traced here: 162 us
  Pallas kernels  160 us (98%)
  local copies, waits for them, and re-layouts  1.88 us (1%)
    pallas_call x1, Pallas kernels, body(): pl.pallas_call(_kernel, out_shape=jax.ShapeDtypeStruct((4, rows, d), BF16...  160 us

profile of v3, /device:TPU:0, one launch (start us, length us, event | category | flops | bytes accessed | tf_op | source)
XLA Modules:
  0.0 162.3 jit_solution(4599977498427762162)
XLA Ops:
  0.0 160.4 %two_layers.1 = bf16[4,32,2048]{2,1,0:T(8,128)(2,1)} custom-call(s32[128]{0:T(128)} %len_ref.1, bf16[4,32,2048]{2,1,0:T(8,128)(2,1)} %bitcast.10, bf16[2,2048]{1,0:T(2,128)(2,1)} %an_ref.1, bf16[2,2048]{1,0:T(2,128)(2,1)} %fn_ref.1, bf16[2,128,576,512]{3,2,1,0:T(8,128)(2,1)} %bitcast.1.cache_hbm, bf16[2,2048,2304]{2,1,0:T(8,128)(2,1)} %wq_hbm.1, ...), custom_call_target="tpu_custom_call" | custom-call | tf_op jit(solution)/shard_map/two_layers/pallas_call | solution.py:393
  160.4 1.9 %copy.12 = bf16[128,2048]{1,0:T(8,128)(2,1)} copy(bf16[128,2048]{1,0:T(8,128)(2,1)} %bitcast.9) | data formatting | bytes 1048576

commit v4 on v3

--- a/solution.py
+++ b/solution.py
@@ -15,13 +15,17 @@
 SCALE = 192 ** -0.5
 VMEM_LIMIT = 64 * 1024 * 1024 - 65536
 
-TP_ORDERS = (('z', 'y'), ('y', 'z'), ('z', 'y'), ('y', 'z'))
+TP_ORDERS = (('z', 'y'), ('y', 'z')) * 4
+GATHER_ORDERS = (
+    ('y', 'z', 'x'), ('z', 'y', 'x'), ('y', 'z', 'x'), ('z', 'y', 'x'),
+    ('y', 'z', 'x'), ('z', 'x', 'y'), ('x', 'y', 'z'), ('x', 'z', 'y'),
+)
 CUBE_ORDERS = (
     ('x', 'y', 'z'), ('y', 'z', 'x'), ('z', 'x', 'y'),
     ('x', 'y', 'z'), ('y', 'z', 'x'), ('z', 'x', 'y'),
     ('x', 'y', 'z'), ('y', 'z', 'x'),
 )
-RING = ((1, 0, 0), (0, 1, 0), (0, 0, 1), (0, 1, 1), (1, 1, 0), (1, 0, 1), (1, 1, 1))
+NEAR = ((1, 0, 0), (0, 1, 0), (0, 0, 1), (0, 1, 1), (1, 1, 0), (1, 0, 1), (1, 1, 1))
 TP_PEERS = ((1, 0), (0, 1), (1, 1))
 
 
@@ -95,6 +99,39 @@
     def finish(self):
         for copy in self.copies.values():
             copy.wait_send()
+
+
+class Doubling:
+    def __init__(self, here, axes, buf, sems, orders):
+        self.here, self.axes, self.buf, self.sems, self.orders = here, axes, buf, sems, orders
+        self.copies = {}
+
+    def send(self, chunk, phase):
+        order = self.orders[chunk]
+        held = order[:phase]
+        part = self.buf.at[(chunk, *(slice(None) if axis in held else self.here.at[axis] for axis in self.axes))]
+        self.copies[chunk, phase] = _send(
+            part, part, self.sems, phase * len(self.orders) + chunk, self.here.along(order[phase]),
+        )
+
+    def wait(self, chunk, phase):
+        self.copies[chunk, phase].wait_recv()
+
+    def finish(self):
+        for copy in self.copies.values():
+            copy.wait_send()
+
+
+def _skewed(count, stages, lag, filler=()):
+    filler = list(filler)
+    for step in range(count + lag * (len(stages) - 1)):
+        for k in reversed(range(len(stages))):
+            if 0 <= step - k * lag < count:
+                stages[k](step - k * lag)
+        if filler:
+            filler.pop(0)()
+    for work in filler:
+        work()
 
 
 def _kernel(
@@ -114,9 +151,12 @@
     heads = o_send.shape[2]
     kv = c_buf.shape[2]
     q_width = q_send.shape[-1] // 3
+    chunks = len(CUBE_ORDERS)
+    width = d // chunks
+    swaps = []
     partner = here.other(dc=1)
     peers = [here.other(dz=dz, dy=dy) for dz, dy in TP_PEERS]
-    cube = [here.other(dx=dx, dz=dz, dy=dy) for dx, dz, dy in RING]
+    cube = [here.other(dx=dx, dz=dz, dy=dy) for dx, dz, dy in NEAR]
 
     def wq_copy(layer, n):
         part = slice(n * q_width, (n + 1) * q_width)
@@ -155,6 +195,30 @@
             pair = pltpu.einshape('alk->lak', stage[slot, r:n])
             w_buf[k, here.c, lo + r:lo + n, :] = pair[layer]
 
+    def share(layer, i):
+        piece_copy(i).wait()
+        unpack(layer, i)
+        if i + ring < len(pieces):
+            piece_copy(i + ring).start()
+        elif layer + 1 < n_layers:
+            piece_copy(i + ring - len(pieces)).start()
+        k = pieces[i][0]
+        if i + 1 == len(pieces) or pieces[i + 1][0] != k:
+            if layer and k == 0:
+                pl.semaphore_wait(credit, 1)
+            mine = w_buf.at[k, here.c]
+            swaps.append(_send(mine, mine, ws_sems, k, partner))
+
+    def exchange(src, dst, sems, i, k):
+        return pltpu.make_async_remote_copy(
+            src_ref=src.at[peers[k]['tp'], i], dst_ref=dst.at[here.tp, i],
+            send_sem=sems.at[0, 3 * i + k], recv_sem=sems.at[1, 3 * i + k],
+            device_id=peers[k], device_id_type=MESH,
+        )
+
+    q_copy = functools.partial(exchange, q_send, q_recv, q_sems)
+    o_copy = functools.partial(exchange, o_send, o_all, o_sems)
+
     for n in range(3):
         wq_copy(0, n).start()
     for i in range(2):
@@ -170,57 +234,35 @@
 
         for t in range(4):
             h_buf[t * rows:(t + 1) * rows, :] = _norm(x_all[t], an_ref[layer:layer + 1, :])
-        q_copies = []
         for n in range(3):
             wq_copy(layer, n).wait()
             part = slice(n * q_width, (n + 1) * q_width)
             q = jnp.dot(h_buf[...], wq_buf[:, part], preferred_element_type=F32).astype(BF16)
-            q_send[:, :, part] = q.reshape(4, rows, q_width)
-            for k, peer in enumerate(peers):
-                q_copies.append(_send(
-                    q_send.at[peer['tp'], :, part], q_recv.at[here.tp, :, part], q_sems, 3 * n + k, peer,
-                ))
+            q_send[:, :, :, part] = q.reshape(4, units, unit, q_width)
+        for i in range(units):
+            for k in range(3):
+                q_copy(i, k).start()
         if not last:
             for n in range(3):
                 wq_copy(layer + 1, n).start()
         q_recv[here.tp] = q_send[here.tp]
 
-        swaps = []
-        for i in range(len(pieces)):
-            piece_copy(i).wait()
-            unpack(layer, i)
-            if i + ring < len(pieces):
-                piece_copy(i + ring).start()
-            k = pieces[i][0]
-            if i + 1 == len(pieces) or pieces[i + 1][0] != k:
-                if layer and k == 0:
-                    pl.semaphore_wait(credit, 1)
-                mine = w_buf.at[k, here.c]
-                swaps.append(_send(mine, mine, ws_sems, k, partner))
-        if not last:
-            for i in range(ring):
-                piece_copy(i).start()
-
-        for copy in q_copies:
-            copy.wait_recv()
-        for h in range(heads):
-            q = q_recv[:, :, h * kv:(h + 1) * kv]
-            q_att[:, 4 * h:4 * h + 4, :] = pltpu.einshape('tbk->btk', q)
-
-        def o_copy(i, k):
-            return pltpu.make_async_remote_copy(
-                src_ref=o_send.at[peers[k]['tp'], i], dst_ref=o_all.at[here.tp, i],
-                send_sem=o_sems.at[0, 3 * i + k], recv_sem=o_sems.at[1, 3 * i + k],
-                device_id=peers[k], device_id_type=MESH,
-            )
+        if layer == 0:
+            for i in range(len(pieces)):
+                share(0, i)
 
         @pl.loop(0, units)
         def _(i):
             slot = lax.rem(i, 2)
+            for k in range(3):
+                q_copy(i, k).wait_recv()
+            for h in range(heads):
+                q = q_recv[:, i, :, h * kv:(h + 1) * kv]
+                q_att[:, 4 * h:4 * h + 4, :] = pltpu.einshape('tbk->btk', q)
             cache_copy(layer, i).wait()
             for lo in range(0, unit, 4):
                 scores = [
-                    jnp.dot(q_att[i * unit + k], c_buf[slot, k], preferred_element_type=F32)
+                    jnp.dot(q_att[k], c_buf[slot, k], preferred_element_type=F32)
                     for k in range(lo, lo + 4)
                 ]
                 probs = []
@@ -255,40 +297,46 @@
             for k in range(3):
                 o_copy(i, k).wait_recv()
 
-        width = p_buf.shape[-1]
         lhs = jnp.concatenate([o_all[:, :, h].reshape(4 * rows, LAT) for h in range(heads)], axis=1)
         attn = Halving(here, ('z', 'y'), p_buf, (pr1, pr2), p_sems, TP_ORDERS)
-        for n in range(len(TP_ORDERS)):
-            part = slice(n * width, (n + 1) * width)
-            p_buf[n] = jnp.dot(lhs, wo_buf[:, part], preferred_element_type=F32).reshape(p_buf.shape[1:])
-            attn.send(n, 0)
+        gather = Doubling(here, ('x', 'z', 'y'), g_all, g_sems, GATHER_ORDERS)
+        for n in range(0, chunks, 2):
+            part = slice(n * width, (n + 2) * width)
+            y = jnp.dot(lhs, wo_buf[:, part], preferred_element_type=F32)
+            for k in range(2):
+                p_buf[n + k] = y[:, k * width:(k + 1) * width].reshape(p_buf.shape[1:])
+                attn.send(n + k, 0)
         if not last:
             wo_copy(layer + 1).start()
-        for n in range(len(TP_ORDERS)):
+        x_mine = x_ref[here.tp] if layer == 0 else x_buf[...]
+
+        def attn_first(n):
             attn.add(n, 0)
             attn.send(n, 1)
-        x_mine = x_ref[here.tp] if layer == 0 else x_buf[...]
-        g_copies = []
-        for n in range(len(TP_ORDERS)):
+
+        def attn_last(n):
             part = slice(n * width, (n + 1) * width)
             total = attn.add(n, 1).astype(BF16)
             x_part = (x_mine[:, part].astype(F32) + total.astype(F32)).astype(BF16)
             x_buf[:, part] = x_part
-            g_all[here.x, here.tp, :, part] = x_part
-            mine = g_all.at[here.x, here.tp, :, part]
-            g_copies.append([_send(mine, mine, g_sems, 7 * n + k, device) for k, device in enumerate(cube)])
-
-        def g_norm(x, t):
-            at = pl.multiple_of((4 * x + t) * rows, rows)
-            g_buf[pl.ds(at, rows), :] = _norm(g_all[x, t], fn_ref[layer:layer + 1, :])
-
-        g_norm(here.x, here.tp)
+            g_all[n, here.x, here.z, here.y] = x_part
+            gather.send(n, 0)
+
+        def pass_on(phase, n):
+            gather.wait(n, phase)
+            if phase < 2:
+                gather.send(n, phase + 1)
+
+        _skewed(chunks, [attn_first, attn_last] + [functools.partial(pass_on, phase) for phase in range(3)], 2)
+
+        for x in range(2):
+            for t in range(4):
+                block = jnp.concatenate([g_all[n, x, t // 2, t % 2] for n in range(chunks)], axis=1)
+                at = (4 * x + t) * rows
+                g_buf[at:at + rows, :] = _norm(block, fn_ref[layer:layer + 1, :])
         for copy in swaps:
-            copy.wait_recv()
-        for k, device in enumerate(cube):
-            for copies in g_copies:
-                copies[k].wait_recv()
-            g_norm(lax.div(device['dp'], 2), device['tp'])
+            copy.wait()
+        swaps.clear()
 
         @pl.loop(0, 2)
         def _(s):
@@ -302,8 +350,7 @@
                 a_buf[s, :, part] = (u * jax.nn.sigmoid(u) * v).T.astype(BF16)
 
         ffn = Halving(here, ('x', 'z', 'y'), y_buf, (yr1, yr2, yr3), y_sems, CUBE_ORDERS)
-        width = y_buf.shape[-1]
-        for n in range(len(CUBE_ORDERS)):
+        for n in range(chunks):
             part = slice(n * width, (n + 1) * width)
             y = jnp.dot(a_buf[0], w_buf[2, 0, :, part], preferred_element_type=F32)
             y += jnp.dot(a_buf[1], w_buf[2, 1, :, part], preferred_element_type=F32)
@@ -311,28 +358,34 @@
             ffn.send(n, 0)
         if not last:
             pl.semaphore_signal(credit, inc=1, device_id=partner, device_id_type=MESH)
-        for phase in range(2):
-            for n in range(len(CUBE_ORDERS)):
-                ffn.add(n, phase)
-                ffn.send(n, phase + 1)
         h_copies = []
-        for n in range(len(CUBE_ORDERS)):
+
+        def ffn_next(phase, n):
+            ffn.add(n, phase)
+            ffn.send(n, phase + 1)
+
+        def ffn_last(n):
             part = slice(n * width, (n + 1) * width)
             total = ffn.add(n, 2).astype(BF16)
             x_part = (x_buf[:, part].astype(F32) + total.astype(F32)).astype(BF16)
             x_buf[:, part] = x_part
             h_all[here.tp, :, part] = x_part
             mine = h_all.at[here.tp, :, part]
-            h_copies += [_send(mine, mine, h_sems, 3 * n + k, peer) for k, peer in enumerate(peers)]
+            h_copies.extend(_send(mine, mine, h_sems, 3 * n + k, peer) for k, peer in enumerate(peers))
+
+        filler = [] if last else [functools.partial(share, layer + 1, i) for i in range(len(pieces))]
+        _skewed(chunks, [functools.partial(ffn_next, 0), functools.partial(ffn_next, 1), ffn_last], 2, filler)
 
         for copy in h_copies:
             copy.wait_recv()
         attn.finish()
+        gather.finish()
         ffn.finish()
-        for copy in q_copies + swaps + h_copies + [copy for copies in g_copies for copy in copies]:
+        for copy in h_copies:
             copy.wait_send()
         for i in range(units):
             for k in range(3):
+                q_copy(i, k).wait_send()
                 o_copy(i, k).wait_send()
     out_ref[...] = h_all[...]
 
@@ -351,7 +404,7 @@
         rows = nb // 4
         cols = w1.shape[2]
         unit = 8
-        q_shape = (4, rows, heads * kv)
+        q_shape = (4, rows // unit, unit, heads * kv)
         scratch = [
             pltpu.VMEM(wq.shape[1:], BF16),
             pltpu.VMEM(wo.shape[1:], BF16),
@@ -361,15 +414,15 @@
             pltpu.VMEM((nb, d), BF16),
             pltpu.VMEM(q_shape, BF16),
             pltpu.VMEM(q_shape, BF16),
-            pltpu.VMEM((rows, 4 * heads, kv), BF16),
+            pltpu.VMEM((unit, 4 * heads, kv), BF16),
             pltpu.VMEM((LAT // 128, unit * 4 * heads, 128), F32),
             pltpu.VMEM((4, rows // unit, heads, unit, LAT), BF16),
             pltpu.VMEM((4, rows // unit, heads, unit, LAT), BF16),
-            pltpu.VMEM((4, 2, 2, rows, d // 4), F32),
-            pltpu.VMEM((4, 2, rows, d // 4), F32),
-            pltpu.VMEM((4, rows, d // 4), F32),
+            pltpu.VMEM((8, 2, 2, rows, d // 8), F32),
+            pltpu.VMEM((8, 2, rows, d // 8), F32),
+            pltpu.VMEM((8, rows, d // 8), F32),
             pltpu.VMEM((rows, d), BF16),
-            pltpu.VMEM((2, 4, rows, d), BF16),
+            pltpu.VMEM((8, 2, 2, 2, rows, d // 8), BF16),
             pltpu.VMEM((8 * rows, d), BF16),
             pltpu.VMEM((2, 8 * rows, cols), BF16),
             pltpu.VMEM((8, 2, 2, 2, rows, d // 8), F32),
@@ -382,10 +435,10 @@
             DMA((2,)),
             DMA((2, 3)),
             DMA((2,)),
-            DMA((2, 9)),
             DMA((2, 12)),
-            DMA((2, 8)),
-            DMA((2, 28)),
+            DMA((2, 12)),
+            DMA((2, 16)),
+            DMA((2, 24)),
             DMA((2, 24)),
             DMA((2, 24)),
             pltpu.SemaphoreType.REGULAR,

time: 163 us -> 185 us (1.13)
  Pallas kernels: 160 us -> 182 us
    pallas_call x1, Pallas kernels: 160 us -> 182 us  [body(): pl.pallas_call(_kernel, out_shape=jax.ShapeDtypeStruct((4, rows, d), BF16...]
where the time goes in v4:
time: 185 us; the launch traced here: 184 us
  Pallas kernels  182 us (98%)
  local copies, waits for them, and re-layouts  1.88 us (1%)
    pallas_call x1, Pallas kernels, body(): pl.pallas_call(_kernel, out_shape=jax.ShapeDtypeStruct((4, rows, d), BF16...  182 us

profile of v4, /device:TPU:0, one launch (start us, length us, event | category | flops | bytes accessed | tf_op | source)
XLA Modules:
  0.0 184.1 jit_solution(9309318434930548410)
XLA Ops:
  0.0 182.2 %two_layers.1 = bf16[4,32,2048]{2,1,0:T(8,128)(2,1)} custom-call(s32[128]{0:T(128)} %len_ref.1, bf16[4,32,2048]{2,1,0:T(8,128)(2,1)} %bitcast.10, bf16[2,2048]{1,0:T(2,128)(2,1)} %an_ref.1, bf16[2,2048]{1,0:T(2,128)(2,1)} %fn_ref.1, bf16[2,128,576,512]{3,2,1,0:T(8,128)(2,1)} %bitcast.1.cache_hbm, bf16[2,2048,2304]{2,1,0:T(8,128)(2,1)} %wq_hbm.1, ...), custom_call_target="tpu_custom_call" | custom-call | tf_op jit(solution)/shard_map/two_layers/pallas_call | solution.py:446
  182.3 1.9 %copy.12 = bf16[128,2048]{1,0:T(8,128)(2,1)} copy(bf16[128,2048]{1,0:T(8,128)(2,1)} %bitcast.9) | data formatting | bytes 1048576

commit v5 on v3

--- a/solution.py
+++ b/solution.py
@@ -15,13 +15,13 @@
 SCALE = 192 ** -0.5
 VMEM_LIMIT = 64 * 1024 * 1024 - 65536
 
-TP_ORDERS = (('z', 'y'), ('y', 'z'), ('z', 'y'), ('y', 'z'))
+TP_ORDERS = (('z', 'y'), ('y', 'z')) * 2
 CUBE_ORDERS = (
     ('x', 'y', 'z'), ('y', 'z', 'x'), ('z', 'x', 'y'),
     ('x', 'y', 'z'), ('y', 'z', 'x'), ('z', 'x', 'y'),
     ('x', 'y', 'z'), ('y', 'z', 'x'),
 )
-RING = ((1, 0, 0), (0, 1, 0), (0, 0, 1), (0, 1, 1), (1, 1, 0), (1, 0, 1), (1, 1, 1))
+NEAR = ((1, 0, 0), (0, 1, 0), (0, 0, 1), (0, 1, 1), (1, 1, 0), (1, 0, 1), (1, 1, 1))
 TP_PEERS = ((1, 0), (0, 1), (1, 1))
 
 
@@ -114,9 +114,12 @@
     heads = o_send.shape[2]
     kv = c_buf.shape[2]
     q_width = q_send.shape[-1] // 3
+    chunks = len(CUBE_ORDERS)
+    width = d // chunks
+    swaps = []
     partner = here.other(dc=1)
     peers = [here.other(dz=dz, dy=dy) for dz, dy in TP_PEERS]
-    cube = [here.other(dx=dx, dz=dz, dy=dy) for dx, dz, dy in RING]
+    cube = [here.other(dx=dx, dz=dz, dy=dy) for dx, dz, dy in NEAR]
 
     def wq_copy(layer, n):
         part = slice(n * q_width, (n + 1) * q_width)
@@ -155,6 +158,30 @@
             pair = pltpu.einshape('alk->lak', stage[slot, r:n])
             w_buf[k, here.c, lo + r:lo + n, :] = pair[layer]
 
+    def share(layer, i):
+        piece_copy(i).wait()
+        unpack(layer, i)
+        if i + ring < len(pieces):
+            piece_copy(i + ring).start()
+        elif layer + 1 < n_layers:
+            piece_copy(i + ring - len(pieces)).start()
+        k = pieces[i][0]
+        if i + 1 == len(pieces) or pieces[i + 1][0] != k:
+            if layer and k == 0:
+                pl.semaphore_wait(credit, 1)
+            mine = w_buf.at[k, here.c]
+            swaps.append(_send(mine, mine, ws_sems, k, partner))
+
+    def exchange(src, dst, sems, i, k):
+        return pltpu.make_async_remote_copy(
+            src_ref=src.at[peers[k]['tp'], i], dst_ref=dst.at[here.tp, i],
+            send_sem=sems.at[0, 3 * i + k], recv_sem=sems.at[1, 3 * i + k],
+            device_id=peers[k], device_id_type=MESH,
+        )
+
+    q_copy = functools.partial(exchange, q_send, q_recv, q_sems)
+    o_copy = functools.partial(exchange, o_send, o_all, o_sems)
+
     for n in range(3):
         wq_copy(0, n).start()
     for i in range(2):
@@ -170,57 +197,35 @@
 
         for t in range(4):
             h_buf[t * rows:(t + 1) * rows, :] = _norm(x_all[t], an_ref[layer:layer + 1, :])
-        q_copies = []
         for n in range(3):
             wq_copy(layer, n).wait()
             part = slice(n * q_width, (n + 1) * q_width)
             q = jnp.dot(h_buf[...], wq_buf[:, part], preferred_element_type=F32).astype(BF16)
-            q_send[:, :, part] = q.reshape(4, rows, q_width)
-            for k, peer in enumerate(peers):
-                q_copies.append(_send(
-                    q_send.at[peer['tp'], :, part], q_recv.at[here.tp, :, part], q_sems, 3 * n + k, peer,
-                ))
+            q_send[:, :, :, part] = q.reshape(4, units, unit, q_width)
+        for i in range(units):
+            for k in range(3):
+                q_copy(i, k).start()
         if not last:
             for n in range(3):
                 wq_copy(layer + 1, n).start()
         q_recv[here.tp] = q_send[here.tp]
 
-        swaps = []
-        for i in range(len(pieces)):
-            piece_copy(i).wait()
-            unpack(layer, i)
-            if i + ring < len(pieces):
-                piece_copy(i + ring).start()
-            k = pieces[i][0]
-            if i + 1 == len(pieces) or pieces[i + 1][0] != k:
-                if layer and k == 0:
-                    pl.semaphore_wait(credit, 1)
-                mine = w_buf.at[k, here.c]
-                swaps.append(_send(mine, mine, ws_sems, k, partner))
-        if not last:
-            for i in range(ring):
-                piece_copy(i).start()
-
-        for copy in q_copies:
-            copy.wait_recv()
-        for h in range(heads):
-            q = q_recv[:, :, h * kv:(h + 1) * kv]
-            q_att[:, 4 * h:4 * h + 4, :] = pltpu.einshape('tbk->btk', q)
-
-        def o_copy(i, k):
-            return pltpu.make_async_remote_copy(
-                src_ref=o_send.at[peers[k]['tp'], i], dst_ref=o_all.at[here.tp, i],
-                send_sem=o_sems.at[0, 3 * i + k], recv_sem=o_sems.at[1, 3 * i + k],
-                device_id=peers[k], device_id_type=MESH,
-            )
+        if layer == 0:
+            for i in range(len(pieces)):
+                share(0, i)
 
         @pl.loop(0, units)
         def _(i):
             slot = lax.rem(i, 2)
+            for k in range(3):
+                q_copy(i, k).wait_recv()
+            for h in range(heads):
+                q = q_recv[:, i, :, h * kv:(h + 1) * kv]
+                q_att[:, 4 * h:4 * h + 4, :] = pltpu.einshape('tbk->btk', q)
             cache_copy(layer, i).wait()
             for lo in range(0, unit, 4):
                 scores = [
-                    jnp.dot(q_att[i * unit + k], c_buf[slot, k], preferred_element_type=F32)
+                    jnp.dot(q_att[k], c_buf[slot, k], preferred_element_type=F32)
                     for k in range(lo, lo + 4)
                 ]
                 probs = []
@@ -255,11 +260,11 @@
             for k in range(3):
                 o_copy(i, k).wait_recv()
 
-        width = p_buf.shape[-1]
+        wide = p_buf.shape[-1]
         lhs = jnp.concatenate([o_all[:, :, h].reshape(4 * rows, LAT) for h in range(heads)], axis=1)
         attn = Halving(here, ('z', 'y'), p_buf, (pr1, pr2), p_sems, TP_ORDERS)
         for n in range(len(TP_ORDERS)):
-            part = slice(n * width, (n + 1) * width)
+            part = slice(n * wide, (n + 1) * wide)
             p_buf[n] = jnp.dot(lhs, wo_buf[:, part], preferred_element_type=F32).reshape(p_buf.shape[1:])
             attn.send(n, 0)
         if not last:
@@ -270,7 +275,7 @@
         x_mine = x_ref[here.tp] if layer == 0 else x_buf[...]
         g_copies = []
         for n in range(len(TP_ORDERS)):
-            part = slice(n * width, (n + 1) * width)
+            part = slice(n * wide, (n + 1) * wide)
             total = attn.add(n, 1).astype(BF16)
             x_part = (x_mine[:, part].astype(F32) + total.astype(F32)).astype(BF16)
             x_buf[:, part] = x_part
@@ -284,7 +289,8 @@
 
         g_norm(here.x, here.tp)
         for copy in swaps:
-            copy.wait_recv()
+            copy.wait()
+        swaps.clear()
         for k, device in enumerate(cube):
             for copies in g_copies:
                 copies[k].wait_recv()
@@ -302,8 +308,7 @@
                 a_buf[s, :, part] = (u * jax.nn.sigmoid(u) * v).T.astype(BF16)
 
         ffn = Halving(here, ('x', 'z', 'y'), y_buf, (yr1, yr2, yr3), y_sems, CUBE_ORDERS)
-        width = y_buf.shape[-1]
-        for n in range(len(CUBE_ORDERS)):
+        for n in range(chunks):
             part = slice(n * width, (n + 1) * width)
             y = jnp.dot(a_buf[0], w_buf[2, 0, :, part], preferred_element_type=F32)
             y += jnp.dot(a_buf[1], w_buf[2, 1, :, part], preferred_element_type=F32)
@@ -312,11 +317,13 @@
         if not last:
             pl.semaphore_signal(credit, inc=1, device_id=partner, device_id_type=MESH)
         for phase in range(2):
-            for n in range(len(CUBE_ORDERS)):
+            for n in range(chunks):
                 ffn.add(n, phase)
                 ffn.send(n, phase + 1)
+                if not last and phase * chunks + n < len(pieces):
+                    share(layer + 1, phase * chunks + n)
         h_copies = []
-        for n in range(len(CUBE_ORDERS)):
+        for n in range(chunks):
             part = slice(n * width, (n + 1) * width)
             total = ffn.add(n, 2).astype(BF16)
             x_part = (x_buf[:, part].astype(F32) + total.astype(F32)).astype(BF16)
@@ -329,10 +336,11 @@
             copy.wait_recv()
         attn.finish()
         ffn.finish()
-        for copy in q_copies + swaps + h_copies + [copy for copies in g_copies for copy in copies]:
+        for copy in h_copies + [copy for copies in g_copies for copy in copies]:
             copy.wait_send()
         for i in range(units):
             for k in range(3):
+                q_copy(i, k).wait_send()
                 o_copy(i, k).wait_send()
     out_ref[...] = h_all[...]
 
@@ -351,7 +359,7 @@
         rows = nb // 4
         cols = w1.shape[2]
         unit = 8
-        q_shape = (4, rows, heads * kv)
+        q_shape = (4, rows // unit, unit, heads * kv)
         scratch = [
             pltpu.VMEM(wq.shape[1:], BF16),
             pltpu.VMEM(wo.shape[1:], BF16),
@@ -361,7 +369,7 @@
             pltpu.VMEM((nb, d), BF16),
             pltpu.VMEM(q_shape, BF16),
             pltpu.VMEM(q_shape, BF16),
-            pltpu.VMEM((rows, 4 * heads, kv), BF16),
+            pltpu.VMEM((unit, 4 * heads, kv), BF16),
             pltpu.VMEM((LAT // 128, unit * 4 * heads, 128), F32),
             pltpu.VMEM((4, rows // unit, heads, unit, LAT), BF16),
             pltpu.VMEM((4, rows // unit, heads, unit, LAT), BF16),
@@ -382,7 +390,7 @@
             DMA((2,)),
             DMA((2, 3)),
             DMA((2,)),
-            DMA((2, 9)),
+            DMA((2, 12)),
             DMA((2, 12)),
             DMA((2, 8)),
             DMA((2, 28)),

time: 163 us -> 157 us (0.963)
  Pallas kernels: 160 us -> 155 us
    pallas_call x1, Pallas kernels: 160 us -> 155 us  [body(): pl.pallas_call(_kernel, out_shape=jax.ShapeDtypeStruct((4, rows, d), BF16...]
where the time goes in v5:
time: 157 us
  Pallas kernels  155 us (99%)
  local copies, waits for them, and re-layouts  1.88 us (1%)
    pallas_call x1, Pallas kernels, body(): pl.pallas_call(_kernel, out_shape=jax.ShapeDtypeStruct((4, rows, d), BF16...  155 us

profile of v5, /device:TPU:0, one launch (start us, length us, event | category | flops | bytes accessed | tf_op | source)
XLA Modules:
  0.0 156.5 jit_solution(7715400988981293929)
XLA Ops:
  0.0 154.6 %two_layers.1 = bf16[4,32,2048]{2,1,0:T(8,128)(2,1)} custom-call(s32[128]{0:T(128)} %len_ref.1, bf16[4,32,2048]{2,1,0:T(8,128)(2,1)} %bitcast.10, bf16[2,2048]{1,0:T(2,128)(2,1)} %an_ref.1, bf16[2,2048]{1,0:T(2,128)(2,1)} %fn_ref.1, bf16[2,128,576,512]{3,2,1,0:T(8,128)(2,1)} %bitcast.1.cache_hbm, bf16[2,2048,2304]{2,1,0:T(8,128)(2,1)} %wq_hbm.1, ...), custom_call_target="tpu_custom_call" | custom-call | tf_op jit(solution)/shard_map/two_layers/pallas_call | solution.py:401
  154.6 1.9 %copy.12 = bf16[128,2048]{1,0:T(8,128)(2,1)} copy(bf16[128,2048]{1,0:T(8,128)(2,1)} %bitcast.9) | data formatting | bytes 1048576

commit v6 on v5

--- a/solution.py
+++ b/solution.py
@@ -22,6 +22,7 @@
     ('x', 'y', 'z'), ('y', 'z', 'x'),
 )
 NEAR = ((1, 0, 0), (0, 1, 0), (0, 0, 1), (0, 1, 1), (1, 1, 0), (1, 0, 1), (1, 1, 1))
+CROSSINGS = ((0, 1, 0), (0, 0, 1), (1, 0, 0), (1, 0, 0))
 TP_PEERS = ((1, 0), (0, 1), (1, 1))
 
 
@@ -62,7 +63,11 @@
     barrier = pltpu.get_barrier_semaphore()
     for device in devices:
         pl.semaphore_signal(barrier, inc=1, device_id=device, device_id_type=MESH)
-    pl.semaphore_wait(barrier, len(devices))
+    return functools.partial(pl.semaphore_wait, barrier, len(devices))
+
+
+def _meet(a, b):
+    return any(p and q for p, q in zip(a, b))
 
 
 class Halving:
@@ -189,7 +194,7 @@
     for i in range(ring):
         piece_copy(i).start()
     wo_copy(0).start()
-    _greet(cube + [partner])
+    greeted = _greet(cube + [partner])
 
     for layer in range(n_layers):
         last = layer + 1 == n_layers
@@ -202,6 +207,8 @@
             part = slice(n * q_width, (n + 1) * q_width)
             q = jnp.dot(h_buf[...], wq_buf[:, part], preferred_element_type=F32).astype(BF16)
             q_send[:, :, :, part] = q.reshape(4, units, unit, q_width)
+        if layer == 0:
+            greeted()
         for i in range(units):
             for k in range(3):
                 q_copy(i, k).start()
@@ -274,14 +281,31 @@
             attn.send(n, 1)
         x_mine = x_ref[here.tp] if layer == 0 else x_buf[...]
         g_copies = []
+
+        def g_send(n, source, target, sem):
+            device = here.other(*source)
+            block = g_all.at[lax.div(device['dp'], 2), device['tp'], :, n * wide:(n + 1) * wide]
+            return _send(block, block, g_sems, 7 * n + NEAR.index(sem), here.other(*target))
+
         for n in range(len(TP_ORDERS)):
             part = slice(n * wide, (n + 1) * wide)
             total = attn.add(n, 1).astype(BF16)
             x_part = (x_mine[:, part].astype(F32) + total.astype(F32)).astype(BF16)
             x_buf[:, part] = x_part
             g_all[here.x, here.tp, :, part] = x_part
-            mine = g_all.at[here.x, here.tp, :, part]
-            g_copies.append([_send(mine, mine, g_sems, 7 * n + k, device) for k, device in enumerate(cube)])
+            axis = CROSSINGS[n]
+            sent = {}
+            for offset in NEAR:
+                if offset == axis or not _meet(offset, axis):
+                    sent[offset] = g_send(n, (0, 0, 0), offset, offset)
+            g_copies.append(sent)
+        for n, sent in enumerate(g_copies):
+            axis = CROSSINGS[n]
+            for offset in NEAR:
+                if not _meet(offset, axis):
+                    sent[offset].wait_recv()
+                    both = tuple(a + b for a, b in zip(offset, axis))
+                    sent[both] = g_send(n, offset, axis, both)
 
         def g_norm(x, t):
             at = pl.multiple_of((4 * x + t) * rows, rows)
@@ -291,10 +315,15 @@
         for copy in swaps:
             copy.wait()
         swaps.clear()
-        for k, device in enumerate(cube):
-            for copies in g_copies:
-                copies[k].wait_recv()
+        for offset, device in zip(NEAR, cube):
+            for n, sent in enumerate(g_copies):
+                if _meet(offset, CROSSINGS[n]):
+                    sent[offset].wait_recv()
             g_norm(lax.div(device['dp'], 2), device['tp'])
+
+        for sent in g_copies:
+            for copy in sent.values():
+                copy.wait_send()
 
         @pl.loop(0, 2)
         def _(s):
@@ -336,7 +365,7 @@
             copy.wait_recv()
         attn.finish()
         ffn.finish()
-        for copy in h_copies + [copy for copies in g_copies for copy in copies]:
+        for copy in h_copies:
             copy.wait_send()
         for i in range(units):
             for k in range(3):

time: 157 us -> 152 us (0.968)
  Pallas kernels: 155 us -> 150 us
    pallas_call x1, Pallas kernels: 155 us -> 150 us  [body(): pl.pallas_call(_kernel, out_shape=jax.ShapeDtypeStruct((4, rows, d), BF16...]
where the time goes in v6:
time: 152 us; the launch traced here: 151 us
  Pallas kernels  150 us (99%)
  local copies, waits for them, and re-layouts  1.88 us (1%)
    pallas_call x1, Pallas kernels, body(): pl.pallas_call(_kernel, out_shape=jax.ShapeDtypeStruct((4, rows, d), BF16...  150 us

profile of v6, /device:TPU:0, one launch (start us, length us, event | category | flops | bytes accessed | tf_op | source)
XLA Modules:
  0.0 151.5 jit_solution(6028704146913247618)
XLA Ops:
  0.0 149.6 %two_layers.1 = bf16[4,32,2048]{2,1,0:T(8,128)(2,1)} custom-call(s32[128]{0:T(128)} %len_ref.1, bf16[4,32,2048]{2,1,0:T(8,128)(2,1)} %bitcast.10, bf16[2,2048]{1,0:T(2,128)(2,1)} %an_ref.1, bf16[2,2048]{1,0:T(2,128)(2,1)} %fn_ref.1, bf16[2,128,576,512]{3,2,1,0:T(8,128)(2,1)} %bitcast.1.cache_hbm, bf16[2,2048,2304]{2,1,0:T(8,128)(2,1)} %wq_hbm.1, ...), custom_call_target="tpu_custom_call" | custom-call | tf_op jit(solution)/shard_map/two_layers/pallas_call | solution.py:430
  149.6 1.9 %copy.12 = bf16[128,2048]{1,0:T(8,128)(2,1)} copy(bf16[128,2048]{1,0:T(8,128)(2,1)} %bitcast.9) | data formatting | bytes 1048576

commit v7 on v6

--- a/solution.py
+++ b/solution.py
@@ -15,14 +15,14 @@
 SCALE = 192 ** -0.5
 VMEM_LIMIT = 64 * 1024 * 1024 - 65536
 
-TP_ORDERS = (('z', 'y'), ('y', 'z')) * 2
+TP_ORDERS = (('z', 'y'), ('y', 'z')) * 4
 CUBE_ORDERS = (
     ('x', 'y', 'z'), ('y', 'z', 'x'), ('z', 'x', 'y'),
     ('x', 'y', 'z'), ('y', 'z', 'x'), ('z', 'x', 'y'),
     ('x', 'y', 'z'), ('y', 'z', 'x'),
 )
 NEAR = ((1, 0, 0), (0, 1, 0), (0, 0, 1), (0, 1, 1), (1, 1, 0), (1, 0, 1), (1, 1, 1))
-CROSSINGS = ((0, 1, 0), (0, 0, 1), (1, 0, 0), (1, 0, 0))
+CROSSINGS = ((0, 1, 0), (0, 0, 1), (1, 0, 0), (1, 0, 0)) * 2
 TP_PEERS = ((1, 0), (0, 1), (1, 1))
 
 
@@ -121,7 +121,7 @@
     q_width = q_send.shape[-1] // 3
     chunks = len(CUBE_ORDERS)
     width = d // chunks
-    swaps = []
+    swaps, h_copies = [], []
     partner = here.other(dc=1)
     peers = [here.other(dz=dz, dy=dy) for dz, dy in TP_PEERS]
     cube = [here.other(dx=dx, dz=dz, dy=dy) for dx, dz, dy in NEAR]
@@ -185,6 +185,14 @@
         )
 
     q_copy = functools.partial(exchange, q_send, q_recv, q_sems)
+    def q_head(n, k):
+        part = slice(n * q_width, (n + 1) * q_width)
+        return pltpu.make_async_remote_copy(
+            src_ref=q_send.at[peers[k]['tp'], 0, :, part], dst_ref=q_recv.at[here.tp, 0, :, part],
+            send_sem=q_sems.at[0, 3 * units + 3 * n + k], recv_sem=q_sems.at[1, 3 * units + 3 * n + k],
+            device_id=peers[k], device_id_type=MESH,
+        )
+
     o_copy = functools.partial(exchange, o_send, o_all, o_sems)
 
     for n in range(3):
@@ -200,16 +208,25 @@
         last = layer + 1 == n_layers
         x_all = x_ref if layer == 0 else h_all
 
-        for t in range(4):
-            h_buf[t * rows:(t + 1) * rows, :] = _norm(x_all[t], an_ref[layer:layer + 1, :])
+        def h_norm(t):
+            at = pl.multiple_of(t * rows, rows)
+            h_buf[pl.ds(at, rows), :] = _norm(x_all[t], an_ref[layer:layer + 1, :])
+
+        h_norm(here.tp)
+        for k, peer in enumerate(peers):
+            for copy in h_copies[k::3]:
+                copy.wait_recv()
+            h_norm(peer['tp'])
         for n in range(3):
             wq_copy(layer, n).wait()
             part = slice(n * q_width, (n + 1) * q_width)
             q = jnp.dot(h_buf[...], wq_buf[:, part], preferred_element_type=F32).astype(BF16)
             q_send[:, :, :, part] = q.reshape(4, units, unit, q_width)
-        if layer == 0:
-            greeted()
-        for i in range(units):
+            if layer == 0 and n == 0:
+                greeted()
+            for k in range(3):
+                q_head(n, k).start()
+        for i in range(1, units):
             for k in range(3):
                 q_copy(i, k).start()
         if not last:
@@ -221,11 +238,17 @@
             for i in range(len(pieces)):
                 share(0, i)
 
+        for n in range(3):
+            for k in range(3):
+                q_head(n, k).wait_recv()
+
         @pl.loop(0, units)
         def _(i):
             slot = lax.rem(i, 2)
-            for k in range(3):
-                q_copy(i, k).wait_recv()
+            @pl.when(i > 0)
+            def _():
+                for k in range(3):
+                    q_copy(i, k).wait_recv()
             for h in range(heads):
                 q = q_recv[:, i, :, h * kv:(h + 1) * kv]
                 q_att[:, 4 * h:4 * h + 4, :] = pltpu.einshape('tbk->btk', q)
@@ -270,10 +293,11 @@
         wide = p_buf.shape[-1]
         lhs = jnp.concatenate([o_all[:, :, h].reshape(4 * rows, LAT) for h in range(heads)], axis=1)
         attn = Halving(here, ('z', 'y'), p_buf, (pr1, pr2), p_sems, TP_ORDERS)
-        for n in range(len(TP_ORDERS)):
-            part = slice(n * wide, (n + 1) * wide)
-            p_buf[n] = jnp.dot(lhs, wo_buf[:, part], preferred_element_type=F32).reshape(p_buf.shape[1:])
-            attn.send(n, 0)
+        for n in range(0, len(TP_ORDERS), 2):
+            y = jnp.dot(lhs, wo_buf[:, n * wide:(n + 2) * wide], preferred_element_type=F32)
+            for k in range(2):
+                p_buf[n + k] = y[:, k * wide:(k + 1) * wide].reshape(p_buf.shape[1:])
+                attn.send(n + k, 0)
         if not last:
             wo_copy(layer + 1).start()
         for n in range(len(TP_ORDERS)):
@@ -361,16 +385,19 @@
             mine = h_all.at[here.tp, :, part]
             h_copies += [_send(mine, mine, h_sems, 3 * n + k, peer) for k, peer in enumerate(peers)]
 
-        for copy in h_copies:
-            copy.wait_recv()
         attn.finish()
         ffn.finish()
         for copy in h_copies:
             copy.wait_send()
         for i in range(units):
             for k in range(3):
+                (q_head(i - 1, k) if i else q_copy(units - 1, k)).wait_send()
+                o_copy(i, k).wait_send()
+        for i in range(1, units - 1):
+            for k in range(3):
                 q_copy(i, k).wait_send()
-                o_copy(i, k).wait_send()
+    for copy in h_copies:
+        copy.wait_recv()
     out_ref[...] = h_all[...]
 
 
@@ -402,9 +429,9 @@
             pltpu.VMEM((LAT // 128, unit * 4 * heads, 128), F32),
             pltpu.VMEM((4, rows // unit, heads, unit, LAT), BF16),
             pltpu.VMEM((4, rows // unit, heads, unit, LAT), BF16),
-            pltpu.VMEM((4, 2, 2, rows, d // 4), F32),
-            pltpu.VMEM((4, 2, rows, d // 4), F32),
-            pltpu.VMEM((4, rows, d // 4), F32),
+            pltpu.VMEM((8, 2, 2, rows, d // 8), F32),
+            pltpu.VMEM((8, 2, rows, d // 8), F32),
+            pltpu.VMEM((8, rows, d // 8), F32),
             pltpu.VMEM((rows, d), BF16),
             pltpu.VMEM((2, 4, rows, d), BF16),
             pltpu.VMEM((8 * rows, d), BF16),
@@ -419,10 +446,10 @@
             DMA((2,)),
             DMA((2, 3)),
             DMA((2,)),
+            DMA((2, 21)),
             DMA((2, 12)),
-            DMA((2, 12)),
-            DMA((2, 8)),
-            DMA((2, 28)),
+            DMA((2, 16)),
+            DMA((2, 56)),
             DMA((2, 24)),
             DMA((2, 24)),
             pltpu.SemaphoreType.REGULAR,

time: 152 us -> 148 us (0.974)
  Pallas kernels: 150 us -> 145 us
    pallas_call x1, Pallas kernels: 150 us -> 145 us  [body(): pl.pallas_call(_kernel, out_shape=jax.ShapeDtypeStruct((4, rows, d), BF16...]
where the time goes in v7:
time: 148 us; the launch traced here: 147 us
  Pallas kernels  145 us (98%)
  local copies, waits for them, and re-layouts  1.88 us (1%)
    pallas_call x1, Pallas kernels, body(): pl.pallas_call(_kernel, out_shape=jax.ShapeDtypeStruct((4, rows, d), BF16...  145 us

profile of v7, /device:TPU:0, one launch (start us, length us, event | category | flops | bytes accessed | tf_op | source)
XLA Modules:
  0.0 147.3 jit_solution(10506005166926963288)
XLA Ops:
  0.0 145.4 %two_layers.1 = bf16[4,32,2048]{2,1,0:T(8,128)(2,1)} custom-call(s32[128]{0:T(128)} %len_ref.1, bf16[4,32,2048]{2,1,0:T(8,128)(2,1)} %bitcast.10, bf16[2,2048]{1,0:T(2,128)(2,1)} %an_ref.1, bf16[2,2048]{1,0:T(2,128)(2,1)} %fn_ref.1, bf16[2,128,576,512]{3,2,1,0:T(8,128)(2,1)} %bitcast.1.cache_hbm, bf16[2,2048,2304]{2,1,0:T(8,128)(2,1)} %wq_hbm.1, ...), custom_call_target="tpu_custom_call" | custom-call | tf_op jit(solution)/shard_map/two_layers/pallas_call | solution.py:457
  145.4 1.9 %copy.12 = bf16[128,2048]{1,0:T(8,128)(2,1)} copy(bf16[128,2048]{1,0:T(8,128)(2,1)} %bitcast.9) | data formatting | bytes 1048576

commit v8 on v7

--- a/solution.py
+++ b/solution.py
@@ -185,14 +185,6 @@
         )
 
     q_copy = functools.partial(exchange, q_send, q_recv, q_sems)
-    def q_head(n, k):
-        part = slice(n * q_width, (n + 1) * q_width)
-        return pltpu.make_async_remote_copy(
-            src_ref=q_send.at[peers[k]['tp'], 0, :, part], dst_ref=q_recv.at[here.tp, 0, :, part],
-            send_sem=q_sems.at[0, 3 * units + 3 * n + k], recv_sem=q_sems.at[1, 3 * units + 3 * n + k],
-            device_id=peers[k], device_id_type=MESH,
-        )
-
     o_copy = functools.partial(exchange, o_send, o_all, o_sems)
 
     for n in range(3):
@@ -222,11 +214,9 @@
             part = slice(n * q_width, (n + 1) * q_width)
             q = jnp.dot(h_buf[...], wq_buf[:, part], preferred_element_type=F32).astype(BF16)
             q_send[:, :, :, part] = q.reshape(4, units, unit, q_width)
-            if layer == 0 and n == 0:
-                greeted()
-            for k in range(3):
-                q_head(n, k).start()
-        for i in range(1, units):
+        if layer == 0:
+            greeted()
+        for i in range(units):
             for k in range(3):
                 q_copy(i, k).start()
         if not last:
@@ -238,17 +228,11 @@
             for i in range(len(pieces)):
                 share(0, i)
 
-        for n in range(3):
-            for k in range(3):
-                q_head(n, k).wait_recv()
-
         @pl.loop(0, units)
         def _(i):
             slot = lax.rem(i, 2)
-            @pl.when(i > 0)
-            def _():
-                for k in range(3):
-                    q_copy(i, k).wait_recv()
+            for k in range(3):
+                q_copy(i, k).wait_recv()
             for h in range(heads):
                 q = q_recv[:, i, :, h * kv:(h + 1) * kv]
                 q_att[:, 4 * h:4 * h + 4, :] = pltpu.einshape('tbk->btk', q)
@@ -391,11 +375,8 @@
             copy.wait_send()
         for i in range(units):
             for k in range(3):
-                (q_head(i - 1, k) if i else q_copy(units - 1, k)).wait_send()
+                q_copy(i, k).wait_send()
                 o_copy(i, k).wait_send()
-        for i in range(1, units - 1):
-            for k in range(3):
-                q_copy(i, k).wait_send()
     for copy in h_copies:
         copy.wait_recv()
     out_ref[...] = h_all[...]
@@ -446,7 +427,7 @@
             DMA((2,)),
             DMA((2, 3)),
             DMA((2,)),
-            DMA((2, 21)),
+            DMA((2, 12)),
             DMA((2, 12)),
             DMA((2, 16)),
             DMA((2, 56)),

time: 148 us -> 149 us (level)
  Pallas kernels: 145 us -> 147 us
where the time goes in v8:
time: 149 us
  Pallas kernels  147 us (99%)
  local copies, waits for them, and re-layouts  1.88 us (1%)
    pallas_call x1, Pallas kernels, body(): pl.pallas_call(_kernel, out_shape=jax.ShapeDtypeStruct((4, rows, d), BF16...  147 us

profile of v8, /device:TPU:0, one launch (start us, length us, event | category | flops | bytes accessed | tf_op | source)
XLA Modules:
  0.0 148.7 jit_solution(3407744683441738323)
XLA Ops:
  0.0 146.8 %two_layers.1 = bf16[4,32,2048]{2,1,0:T(8,128)(2,1)} custom-call(s32[128]{0:T(128)} %len_ref.1, bf16[4,32,2048]{2,1,0:T(8,128)(2,1)} %bitcast.10, bf16[2,2048]{1,0:T(2,128)(2,1)} %an_ref.1, bf16[2,2048]{1,0:T(2,128)(2,1)} %fn_ref.1, bf16[2,128,576,512]{3,2,1,0:T(8,128)(2,1)} %bitcast.1.cache_hbm, bf16[2,2048,2304]{2,1,0:T(8,128)(2,1)} %wq_hbm.1, ...), custom_call_target="tpu_custom_call" | custom-call | tf_op jit(solution)/shard_map/two_layers/pallas_call | solution.py:438
  146.8 1.9 %copy.12 = bf16[128,2048]{1,0:T(8,128)(2,1)} copy(bf16[128,2048]{1,0:T(8,128)(2,1)} %bitcast.9) | data formatting | bytes 1048576
